TPU v7x, 256 devices: a whole 4x4x8 slice. The times are simulated.
256 devices in a mesh: blk: 128 (over x_lo, z, y, core), aux: 2 (over x_hi).
Axes of the slice: x: 4 (x_hi: 2, x_lo: 2; x = x_hi * 2 + x_lo), y: 4, z: 8, core: 2. Of those that a mesh axis runs over, the one named last changes fastest.
Arguments:
- panels: bfloat16 [4, 11264, 120, 120], P(None, ('blk', 'aux')), may hold values from -0.19921875 to 0.19921875
- aux_counts: int32 [256], replicated, may hold values from 1 to 44, 9000 in all
- pair_list: int32 [512, 2], replicated, may hold values from 0 to 3
- pair_ranks: int32 [512], replicated, may hold values from 24 to 120
- amplitudes: bfloat16 [512, 120, 120], P('blk'), may hold values from -6 to 6
Outputs:
- residual: float32 [512, 120, 120], P('blk', 'aux')
Inputs may be any that keep to these rules, and one draw needn't show every extreme that they name: `aux_counts`: entry k counts the live auxiliary functions of panel shard k (slots k * 44 onward), which come first in the shard; the entries sum to 9000.
All inputs are finite; a program needn't handle non-finite values.
Results may differ from a plain program's by a relative error of at most 0.0029.
Values may be sent and summed in bfloat16 or wider, within the bound.
No kernel may reach another device: no remote copies, remote signals or barrier semaphores. Data moves between devices by JAX's collectives and lax.ppermute only.
A program may use at most 64 MiB of HBM per device.

v0:
```python
import jax
import jax.numpy as jnp
from jax import lax
from jax.sharding import PartitionSpec as P


def passed_along(value, axis, steps):
    count = lax.axis_size(axis)
    pairs = [(source, (source + steps) % count) for source in range(count)]
    return lax.ppermute(value, axis, pairs)


def in_blocks(shard, dim, devices):
    lengths = shard.shape
    parts = shard.reshape(*lengths[:dim], devices, lengths[dim] // devices, *lengths[dim + 1 :])
    return jnp.moveaxis(parts, dim, 0)


def sent_and_summed(shard, axis, dim):
    devices = lax.axis_size(axis)
    parts = lax.all_to_all(in_blocks(shard, dim, devices), axis, 0, 0, tiled=True)
    return jnp.sum(parts, axis=0)


def ladder(block, count, pair_rows, rank_rows, amp_rows):
    slot_count = block.shape[1]
    pno_width = block.shape[2]
    live_slots = jnp.arange(slot_count, dtype=jnp.int32) < count
    positions = jnp.arange(pno_width, dtype=jnp.int32)

    def one_pair(pair_item):
        orbitals, rank_value, pair_amps = pair_item
        kept_mask = positions < rank_value
        pair_mask = kept_mask[:, None] & kept_mask[None, :]
        masked = jnp.where(pair_mask, pair_amps, jnp.zeros_like(pair_amps))
        left_panel = lax.dynamic_index_in_dim(block, orbitals[0], 0, keepdims=False)
        right_panel = lax.dynamic_index_in_dim(block, orbitals[1], 0, keepdims=False)
        half_step = jnp.einsum(
            "sac,cd->sad", left_panel, masked, preferred_element_type=jnp.float32
        )
        half_step = jnp.where(
            live_slots[:, None, None], half_step, jnp.zeros_like(half_step)
        ).astype(jnp.bfloat16)
        ladder_sum = jnp.einsum(
            "sad,sbd->ab", half_step, right_panel, preferred_element_type=jnp.float32
        )
        return jnp.where(pair_mask, ladder_sum, jnp.zeros_like(ladder_sum))

    return lax.map(one_pair, (pair_rows, rank_rows, amp_rows))


def shards(panels, aux_counts, pair_list, pair_ranks, amplitudes):
    cycle_size = lax.axis_size("blk")
    split_size = lax.axis_size("aux")
    cycle_index = lax.axis_index("blk")
    split_index = lax.axis_index("aux")
    pair_count = amplitudes.shape[0]

    def counts_for():
        source = cycle_index % cycle_size
        return aux_counts[source * split_size + split_index]

    def owned(offset):
        start = (cycle_index - offset) % cycle_size * pair_count
        return (
            lax.dynamic_slice_in_dim(pair_list, start, pair_count, 0),
            lax.dynamic_slice_in_dim(pair_ranks, start, pair_count, 0),
        )

    own_pairs, own_ranks = owned(0)
    ladder_sum = ladder(panels, counts_for(), own_pairs, own_ranks, amplitudes)
    near_amps = passed_along(amplitudes, "blk", -1)
    far_amps = passed_along(amplitudes, "blk", -2)
    near_pairs, near_ranks = owned(-1)
    far_pairs, far_ranks = owned(-2)
    near_term = ladder(panels, counts_for(), near_pairs, near_ranks, near_amps)
    far_term = ladder(panels, counts_for(), far_pairs, far_ranks, far_amps)
    ladder_sum = ladder_sum + passed_along(near_term, "blk", 1)
    ladder_sum = ladder_sum + passed_along(far_term, "blk", 2)
    return sent_and_summed(ladder_sum, "aux", 1)


def solution(mesh):
    placed = (P(None, ("blk", "aux"), None, None), P(), P(), P(), P("blk", None, None))
    return jax.shard_map(
        shards, mesh=mesh, in_specs=placed, out_specs=P("blk", "aux", None), check_vma=False
    )
```

profile of v0, /device:TPU:1, one launch (start us, length us, event | category | flops | bytes accessed | tf_op | source)
XLA Modules:
  0.0 140.6 jit_solution(13258579887888965644)
XLA Ops:
  0.0 3.2 %collective-permute-start = (bf16[4,120,120]{2,1,0:T(8,128)(2,1)}, bf16[4,120,120]{2,1,0:T(8,128)(2,1)S(1)}, u32[]{:S(2)}, u32[]{:S(2)}) collective-permute-start(bf16[4,120,120]{2,1,0:T(8,128)(2,1)} %param.15), channel_id=1, source_target_pairs={{0,254},{2,0},{4,2},{6,4},{8,6},{10,8},{12,10},{14,12},{16,14},{18... | collective-permute-start | bytes 345608 | tf_op jit(solution)/shard_map/ppermute | solution.py:10
  3.2 7.2 %collective-permute-start.2 = (bf16[4,120,120]{2,1,0:T(8,128)(2,1)}, bf16[4,120,120]{2,1,0:T(8,128)(2,1)S(1)}, u32[]{:S(2)}, u32[]{:S(2)}) collective-permute-start(bf16[4,120,120]{2,1,0:T(8,128)(2,1)} %param.15), channel_id=1, source_target_pairs={{0,252},{2,254},{4,0},{6,2},{8,4},{10,6},{12,8},{14,10},{16,12},{1... | collective-permute-start | bytes 345608 | tf_op jit(solution)/shard_map/ppermute | solution.py:10
  10.4 0.9 fusion.150
  11.3 1.3 dynamic_slice.73
  12.6 0.9 constant_dynamic-slice_fusion.4
  13.5 37.7 %while.34 = (s32[]{:T(128)}, f32[4,120,120]{2,1,0:T(8,128)S(1)}, s32[4]{0:T(128)S(1)}, s32[4,2]{0,1:T(2,128)S(1)}, bf16[4,44,120,120]{3,2,1,0:T(8,128)(2,1)}, /*...) while((s32[]{:T(128)}, f32[4,120,120]{2,1,0:T(8,128)S(1)}, ...), condition=%wide.region_3.4_spmd.clone, body=%wide.region_2.3_spmd.clone.sunk | while | flops 305452960 | bytes 2799501 | solution.py:49
  17.7 0.6 dynamic_slice.217
  18.4 0.6 iota_compare_fusion.15
  19.0 0.6 iota_compare_fusion.14
  19.6 3.3 %fusion.175 = f32[4,120,120]{2,1,0:T(8,128)S(1)} fusion(f32[4,120,120]{2,1,0:T(8,128)S(1)} %get-tuple-element.454, s32[]{:T(128)} %get-tuple-element.453, bf16[4,44,120,120]{3,2,1,0:T(8,128)(2,1)} %get-tuple-element.467, s32[]{:T(128)S(6)} %select_n.207, s32[]{:T(128)S(6)} %select_n.208, pred[44]{0:T(512)(128)(4,1)S(1)} %iota_compare_fusion.14, ...), kind=kOutput, calls=%fused_computation.41.clone.1 | convolution fusion | flops 305452800 | bytes 2799112 | tf_op jit(solution)/shard_map/while/body/eval_jaxpr/sad,sbd->ab/dot_general | solution.py:44
  27.2 0.6 dynamic_slice.217
  27.8 0.6 iota_compare_fusion.15
  28.4 0.6 iota_compare_fusion.14
  29.1 3.3 %fusion.175 = f32[4,120,120]{2,1,0:T(8,128)S(1)} fusion(f32[4,120,120]{2,1,0:T(8,128)S(1)} %get-tuple-element.454, s32[]{:T(128)} %get-tuple-element.453, bf16[4,44,120,120]{3,2,1,0:T(8,128)(2,1)} %get-tuple-element.467, s32[]{:T(128)S(6)} %select_n.207, s32[]{:T(128)S(6)} %select_n.208, pred[44]{0:T(512)(128)(4,1)S(1)} %iota_compare_fusion.14, ...), kind=kOutput, calls=%fused_computation.41.clone.1 | convolution fusion | flops 305452800 | bytes 2799112 | tf_op jit(solution)/shard_map/while/body/eval_jaxpr/sad,sbd->ab/dot_general | solution.py:44
  36.6 0.6 dynamic_slice.217
  37.2 0.6 iota_compare_fusion.15
  37.8 0.6 iota_compare_fusion.14
  38.5 3.3 %fusion.175 = f32[4,120,120]{2,1,0:T(8,128)S(1)} fusion(f32[4,120,120]{2,1,0:T(8,128)S(1)} %get-tuple-element.454, s32[]{:T(128)} %get-tuple-element.453, bf16[4,44,120,120]{3,2,1,0:T(8,128)(2,1)} %get-tuple-element.467, s32[]{:T(128)S(6)} %select_n.207, s32[]{:T(128)S(6)} %select_n.208, pred[44]{0:T(512)(128)(4,1)S(1)} %iota_compare_fusion.14, ...), kind=kOutput, calls=%fused_computation.41.clone.1 | convolution fusion | flops 305452800 | bytes 2799112 | tf_op jit(solution)/shard_map/while/body/eval_jaxpr/sad,sbd->ab/dot_general | solution.py:44
  46.0 0.6 dynamic_slice.217
  46.6 0.6 iota_compare_fusion.15
  47.3 0.6 iota_compare_fusion.14
  47.9 3.3 %fusion.175 = f32[4,120,120]{2,1,0:T(8,128)S(1)} fusion(f32[4,120,120]{2,1,0:T(8,128)S(1)} %get-tuple-element.454, s32[]{:T(128)} %get-tuple-element.453, bf16[4,44,120,120]{3,2,1,0:T(8,128)(2,1)} %get-tuple-element.467, s32[]{:T(128)S(6)} %select_n.207, s32[]{:T(128)S(6)} %select_n.208, pred[44]{0:T(512)(128)(4,1)S(1)} %iota_compare_fusion.14, ...), kind=kOutput, calls=%fused_computation.41.clone.1 | convolution fusion | flops 305452800 | bytes 2799112 | tf_op jit(solution)/shard_map/while/body/eval_jaxpr/sad,sbd->ab/dot_general | solution.py:44
  51.2 1.5 %collective-permute-start.1 = (f32[4,120,120]{2,1,0:T(8,128)S(1)}, f32[4,120,120]{2,1,0:T(8,128)S(1)}, u32[]{:S(2)}, u32[]{:S(2)}) collective-permute-start(f32[4,120,120]{2,1,0:T(8,128)S(1)} %get-tuple-element.132), channel_id=1, source_target_pairs={{0,2},{2,4},{4,6},{6,8},{8,10},{10,12},{12,14},{14,16},{16,18},{18... | collective-permute-start | bytes 691208 | tf_op jit(solution)/shard_map/ppermute | solution.py:10
  52.7 38.7 %while.35 = (s32[]{:T(128)}, f32[4,120,120]{2,1,0:T(8,128)S(1)}, s32[4]{0:T(128)S(1)}, s32[4,2]{0,1:T(2,128)S(1)}, bf16[4,44,120,120]{3,2,1,0:T(8,128)(2,1)}, /*...) while((s32[]{:T(128)}, f32[4,120,120]{2,1,0:T(8,128)S(1)}, ...), condition=%wide.region_5.6_spmd.clone, body=%wide.region_4.5_spmd.clone.sunk | while | flops 305452960 | bytes 2799501 | solution.py:49
  52.8 0.6 fusion.179
  57.2 0.7 dynamic_slice.222
  57.8 0.6 iota_compare_fusion.17
  58.4 0.6 iota_compare_fusion.16
  59.1 3.3 %fusion.180 = f32[4,120,120]{2,1,0:T(8,128)S(1)} fusion(f32[4,120,120]{2,1,0:T(8,128)S(1)} %get-tuple-element.394, s32[]{:T(128)} %get-tuple-element.393, bf16[4,44,120,120]{3,2,1,0:T(8,128)(2,1)} %get-tuple-element.407, s32[]{:T(128)S(6)} %select_n.212, s32[]{:T(128)S(6)} %select_n.213, pred[44]{0:T(512)(128)(4,1)S(1)} %iota_compare_fusion.16, ...), kind=kOutput, calls=%fused_computation.65.clone.1 | convolution fusion | flops 305452800 | bytes 2799112 | tf_op jit(solution)/shard_map/while/body/eval_jaxpr/sad,sbd->ab/dot_general | solution.py:44
  66.8 0.7 dynamic_slice.222
  67.5 0.6 iota_compare_fusion.17
  68.1 0.6 iota_compare_fusion.16
  68.8 3.3 %fusion.180 = f32[4,120,120]{2,1,0:T(8,128)S(1)} fusion(f32[4,120,120]{2,1,0:T(8,128)S(1)} %get-tuple-element.394, s32[]{:T(128)} %get-tuple-element.393, bf16[4,44,120,120]{3,2,1,0:T(8,128)(2,1)} %get-tuple-element.407, s32[]{:T(128)S(6)} %select_n.212, s32[]{:T(128)S(6)} %select_n.213, pred[44]{0:T(512)(128)(4,1)S(1)} %iota_compare_fusion.16, ...), kind=kOutput, calls=%fused_computation.65.clone.1 | convolution fusion | flops 305452800 | bytes 2799112 | tf_op jit(solution)/shard_map/while/body/eval_jaxpr/sad,sbd->ab/dot_general | solution.py:44
  76.5 0.7 dynamic_slice.222
  77.2 0.6 iota_compare_fusion.17
  77.8 0.6 iota_compare_fusion.16
  78.5 3.3 %fusion.180 = f32[4,120,120]{2,1,0:T(8,128)S(1)} fusion(f32[4,120,120]{2,1,0:T(8,128)S(1)} %get-tuple-element.394, s32[]{:T(128)} %get-tuple-element.393, bf16[4,44,120,120]{3,2,1,0:T(8,128)(2,1)} %get-tuple-element.407, s32[]{:T(128)S(6)} %select_n.212, s32[]{:T(128)S(6)} %select_n.213, pred[44]{0:T(512)(128)(4,1)S(1)} %iota_compare_fusion.16, ...), kind=kOutput, calls=%fused_computation.65.clone.1 | convolution fusion | flops 305452800 | bytes 2799112 | tf_op jit(solution)/shard_map/while/body/eval_jaxpr/sad,sbd->ab/dot_general | solution.py:44
  86.2 0.7 dynamic_slice.222
  86.9 0.6 iota_compare_fusion.17
  87.5 0.6 iota_compare_fusion.16
  88.1 3.3 %fusion.180 = f32[4,120,120]{2,1,0:T(8,128)S(1)} fusion(f32[4,120,120]{2,1,0:T(8,128)S(1)} %get-tuple-element.394, s32[]{:T(128)} %get-tuple-element.393, bf16[4,44,120,120]{3,2,1,0:T(8,128)(2,1)} %get-tuple-element.407, s32[]{:T(128)S(6)} %select_n.212, s32[]{:T(128)S(6)} %select_n.213, pred[44]{0:T(512)(128)(4,1)S(1)} %iota_compare_fusion.16, ...), kind=kOutput, calls=%fused_computation.65.clone.1 | convolution fusion | flops 305452800 | bytes 2799112 | tf_op jit(solution)/shard_map/while/body/eval_jaxpr/sad,sbd->ab/dot_general | solution.py:44
  91.6 38.8 %while.33 = (s32[]{:T(128)}, f32[4,120,120]{2,1,0:T(8,128)S(1)}, s32[4]{0:T(128)S(1)}, s32[4,2]{0,1:T(2,128)S(1)}, bf16[4,44,120,120]{3,2,1,0:T(8,128)(2,1)}, /*...) while((s32[]{:T(128)}, f32[4,120,120]{2,1,0:T(8,128)S(1)}, ...), condition=%wide.region_1.2_spmd.clone, body=%wide.region_0.1_spmd.clone.sunk | while | flops 305452960 | bytes 2799501 | solution.py:49
  91.7 0.6 fusion.169
  96.1 0.6 dynamic_slice.212
  96.6 0.6 iota_compare_fusion.13
  97.3 0.6 iota_compare_fusion.12
  97.9 3.3 %fusion.170 = f32[4,120,120]{2,1,0:T(8,128)S(1)} fusion(f32[4,120,120]{2,1,0:T(8,128)S(1)} %get-tuple-element.424, s32[]{:T(128)} %get-tuple-element.423, bf16[4,44,120,120]{3,2,1,0:T(8,128)(2,1)} %get-tuple-element.437, s32[]{:T(128)S(6)} %select_n.202, s32[]{:T(128)S(6)} %select_n.203, pred[44]{0:T(512)(128)(4,1)S(1)} %iota_compare_fusion.12, ...), kind=kOutput, calls=%fused_computation.17.clone.1 | convolution fusion | flops 305452800 | bytes 2799112 | tf_op jit(solution)/shard_map/while/body/eval_jaxpr/sad,sbd->ab/dot_general | solution.py:44
  101.3 0.6 fusion.169
  105.7 0.6 dynamic_slice.212
  106.3 0.6 iota_compare_fusion.13
  107.0 0.6 iota_compare_fusion.12
  107.6 3.3 %fusion.170 = f32[4,120,120]{2,1,0:T(8,128)S(1)} fusion(f32[4,120,120]{2,1,0:T(8,128)S(1)} %get-tuple-element.424, s32[]{:T(128)} %get-tuple-element.423, bf16[4,44,120,120]{3,2,1,0:T(8,128)(2,1)} %get-tuple-element.437, s32[]{:T(128)S(6)} %select_n.202, s32[]{:T(128)S(6)} %select_n.203, pred[44]{0:T(512)(128)(4,1)S(1)} %iota_compare_fusion.12, ...), kind=kOutput, calls=%fused_computation.17.clone.1 | convolution fusion | flops 305452800 | bytes 2799112 | tf_op jit(solution)/shard_map/while/body/eval_jaxpr/sad,sbd->ab/dot_general | solution.py:44
  111.0 0.6 fusion.169
  115.4 0.6 dynamic_slice.212
  116.0 0.6 iota_compare_fusion.13
  116.7 0.6 iota_compare_fusion.12
  117.3 3.3 %fusion.170 = f32[4,120,120]{2,1,0:T(8,128)S(1)} fusion(f32[4,120,120]{2,1,0:T(8,128)S(1)} %get-tuple-element.424, s32[]{:T(128)} %get-tuple-element.423, bf16[4,44,120,120]{3,2,1,0:T(8,128)(2,1)} %get-tuple-element.437, s32[]{:T(128)S(6)} %select_n.202, s32[]{:T(128)S(6)} %select_n.203, pred[44]{0:T(512)(128)(4,1)S(1)} %iota_compare_fusion.12, ...), kind=kOutput, calls=%fused_computation.17.clone.1 | convolution fusion | flops 305452800 | bytes 2799112 | tf_op jit(solution)/shard_map/while/body/eval_jaxpr/sad,sbd->ab/dot_general | solution.py:44
  120.7 0.6 fusion.169
  125.1 0.6 dynamic_slice.212
  125.7 0.6 iota_compare_fusion.13
  126.4 0.6 iota_compare_fusion.12
  127.0 3.3 %fusion.170 = f32[4,120,120]{2,1,0:T(8,128)S(1)} fusion(f32[4,120,120]{2,1,0:T(8,128)S(1)} %get-tuple-element.424, s32[]{:T(128)} %get-tuple-element.423, bf16[4,44,120,120]{3,2,1,0:T(8,128)(2,1)} %get-tuple-element.437, s32[]{:T(128)S(6)} %select_n.202, s32[]{:T(128)S(6)} %select_n.203, pred[44]{0:T(512)(128)(4,1)S(1)} %iota_compare_fusion.12, ...), kind=kOutput, calls=%fused_computation.17.clone.1 | convolution fusion | flops 305452800 | bytes 2799112 | tf_op jit(solution)/shard_map/while/body/eval_jaxpr/sad,sbd->ab/dot_general | solution.py:44
  130.5 9.4 %all_to_all.5 = f32[2,4,60,120]{3,1,2,0:T(4,128)S(1)} all-to-all(f32[2,4,60,120]{3,1,2,0:T(4,128)S(1)} %bitcast.181), channel_id=1, replica_groups=mesh['blk'=128,'aux'=2] {'aux'}, dimensions={0} | all-to-all | bytes 460800 | tf_op jit(solution)/shard_map/all_to_all | solution.py:21
  139.9 0.7 reduce_sum.9
  (29 shorter events, 5.0 us)
Async XLA Ops:
  0.0 13.5 %collective-permute-start = (bf16[4,120,120]{2,1,0:T(8,128)(2,1)}, bf16[4,120,120]{2,1,0:T(8,128)(2,1)S(1)}, u32[]{:S(2)}, u32[]{:S(2)}) collective-permute-start(bf16[4,120,120]{2,1,0:T(8,128)(2,1)} %param.15), channel_id=1, source_target_pairs={{0,254},{2,0},{4,2},{6,4},{8,6},{10,8},{12,10},{14,12},{16,14},{18... | collective-permute-start | bytes 345608 | tf_op jit(solution)/shard_map/ppermute | solution.py:10
  3.2 49.5 %collective-permute-start.2 = (bf16[4,120,120]{2,1,0:T(8,128)(2,1)}, bf16[4,120,120]{2,1,0:T(8,128)(2,1)S(1)}, u32[]{:S(2)}, u32[]{:S(2)}) collective-permute-start(bf16[4,120,120]{2,1,0:T(8,128)(2,1)} %param.15), channel_id=1, source_target_pairs={{0,252},{2,254},{4,0},{6,2},{8,4},{10,6},{12,8},{14,10},{16,12},{1... | collective-permute-start | bytes 345608 | tf_op jit(solution)/shard_map/ppermute | solution.py:10
  51.2 79.1 %collective-permute-start.1 = (f32[4,120,120]{2,1,0:T(8,128)S(1)}, f32[4,120,120]{2,1,0:T(8,128)S(1)}, u32[]{:S(2)}, u32[]{:S(2)}) collective-permute-start(f32[4,120,120]{2,1,0:T(8,128)S(1)} %get-tuple-element.132), channel_id=1, source_target_pairs={{0,2},{2,4},{4,6},{6,8},{8,10},{10,12},{12,14},{14,16},{16,18},{18... | collective-permute-start | bytes 691208 | tf_op jit(solution)/shard_map/ppermute | solution.py:10
  91.5 38.9 %collective-permute-start.3 = (f32[4,120,120]{2,1,0:T(8,128)S(1)}, f32[4,120,120]{2,1,0:T(8,128)S(1)}, u32[]{:S(2)}, u32[]{:S(2)}) collective-permute-start(f32[4,120,120]{2,1,0:T(8,128)S(1)} %get-tuple-element.133), channel_id=1, source_target_pairs={{0,4},{2,6},{4,8},{6,10},{8,12},{10,14},{12,16},{14,18},{16,20},{1... | collective-permute-start | bytes 691208 | tf_op jit(solution)/shard_map/ppermute | solution.py:10
where the time goes:
time: 142 us; the launch traced here: 141 us
  loops' own time  45.1 us (32%)
  matrix products  39.7 us (28%)
  local copies, waits for them, and re-layouts  18.3 us (13%)
  other arithmetic  16 us (11%)
  starting transfers between devices  12 us (8%)
  blocking collectives  9.42 us (7%)
    another operation x3, loops' own time, ladder(): return lax.map(one_pair, (pair_rows, rank_rows, amp_rows))  45.1 us
    dot_general x12, matrix products, one_pair(): jnp.einsum('sad,sbd->ab', half_step, right_panel, preferred_element_type=...  39.7 us
    ppermute x4, starting transfers between devices, passed_along(): return lax.ppermute(value, axis, pairs)  12 us
    all_to_all x1, blocking collectives, sent_and_summed(): lax.all_to_all(in_blocks(shard, dim, devices), axis, 0, 0, tiled=True)  9.42 us
    dynamic_slice x24, local copies, waits for them, and re-layouts, ladder(): return lax.map(one_pair, (pair_rows, rank_rows, amp_rows))  8.3 us
    lt x12, other arithmetic, one_pair(): kept_mask = positions < rank_value  7.64 us
    lt x12, other arithmetic, ladder(): live_slots = jnp.arange(slot_count, dtype=jnp.int32) < count  7.55 us
    slice x12, local copies, waits for them, and re-layouts, one_pair(): left_panel = lax.dynamic_index_in_dim(block, orbitals[0], 0, keepdims=False)  6.82 us
  transfers between devices with their start and end apart: 4, of which 0 were waited for; matrix products, arithmetic and copies ran while one was open for 52% of the time, Pallas kernels for 0%

commit v1 on v0

v1 whole, which is shorter than its diff:
```python
import functools
import jax
import jax.numpy as jnp
from jax import lax
from jax.experimental import pallas as pl
from jax.experimental.pallas import tpu as pltpu
from jax.sharding import PartitionSpec as P

F32, BF16 = jnp.float32, jnp.bfloat16
SLAB = 128
WIDE = 256
STEP = 2


def meta_copies(counts, pairs, ranks, counts_s, pairs_s, ranks_s, sems):
    return [
        pltpu.make_async_copy(counts, counts_s, sems.at[0]),
        pltpu.make_async_copy(pairs, pairs_s, sems.at[1]),
        pltpu.make_async_copy(ranks, ranks_s, sems.at[2]),
    ]


def one_pair(row, amps, put, paired, both, pairs_s, ranks_s, width):
    left, right, rank = pairs_s[0, row], pairs_s[1, row], ranks_s[row]
    rows = lax.broadcasted_iota(jnp.int32, (width, width), 0)
    cols = lax.broadcasted_iota(jnp.int32, (width, width), 1)
    keep = (rows < rank) & (cols < rank)
    masked = jnp.where(keep, amps, jnp.zeros_like(amps))
    both[0:width, 0:width] = masked
    both[SLAB : SLAB + width, SLAB : SLAB + width] = masked
    total = jnp.zeros((SLAB, SLAB), F32)
    slot_pairs = paired.shape[1]
    for first in range(0, slot_pairs, STEP):
        taken = min(STEP, slot_pairs - first)
        lhs = paired[left, first : first + taken].reshape(taken * SLAB, WIDE)
        half = jnp.dot(lhs, both[...], preferred_element_type=F32)
        for k in range(taken):
            part = half[k * SLAB : (k + 1) * SLAB].astype(BF16)
            total = total + lax.dot_general(
                part, paired[right, first + k], (((1,), (1,)), ((), ())), preferred_element_type=F32
            )
    put(jnp.where(keep, total[:width, :width], 0.0))


def own_body(counts, pairs, ranks, amps, panels, out, paired, raw, both, counts_s, pairs_s, ranks_s, sems, meta_sems):
    orbitals, slots, width, _ = panels.shape
    owned = amps.shape[0]
    cut = width // 2
    block = lax.axis_index("blk")
    shard = block * lax.axis_size("aux") + lax.axis_index("aux")
    copies = [pltpu.make_async_copy(panels.at[o], raw.at[o], sems.at[o]) for o in range(orbitals)]
    for copy in copies:
        copy.start()
    small = meta_copies(counts, pairs, ranks, counts_s, pairs_s, ranks_s, meta_sems)
    for copy in small:
        copy.start()
    both[...] = jnp.zeros_like(both)
    for copy in small:
        copy.wait()
    live = counts_s[shard]
    for o in range(orbitals):
        copies[o].wait()

        def widen(t, carry):
            for side in range(2):
                slot = 2 * t + side
                slab = raw[o, slot]
                slab = jnp.where(slot < live, slab, jnp.zeros_like(slab))
                slab = jnp.pad(slab, ((0, SLAB - width), (0, SLAB - width)))
                paired[o, t, :, side * SLAB : (side + 1) * SLAB] = slab
            return carry

        lax.fori_loop(0, slots // 2, widen, 0, unroll=2)

    def pair(p, carry):
        def put(value):
            out[0, p] = value[:cut]
            out[1, p] = value[cut:]

        one_pair(block * owned + p, amps[p], put, paired, both, pairs_s, ranks_s, width)
        return carry

    lax.fori_loop(0, owned, pair, 0)


def other_body(pairs, ranks, near, far, paired, near_out, far_out, both, pairs_s, ranks_s, meta_sems):
    owned, width, _ = near.shape
    cut = width // 2
    blocks = lax.axis_size("blk")
    block = lax.axis_index("blk")
    small = [
        pltpu.make_async_copy(pairs, pairs_s, meta_sems.at[0]),
        pltpu.make_async_copy(ranks, ranks_s, meta_sems.at[1]),
    ]
    for copy in small:
        copy.start()
    both[...] = jnp.zeros_like(both)
    for copy in small:
        copy.wait()
    for amps, out, hops in ((far, far_out, 2), (near, near_out, 1)):
        start = (block + hops) % blocks * owned

        def pair(p, carry):
            def put(value):
                out[0, p] = value[:cut].astype(BF16)
                out[1, p] = value[cut:].astype(BF16)

            one_pair(start + p, amps[p], put, paired, both, pairs_s, ranks_s, width)
            return carry

        lax.fori_loop(0, owned, pair, 0)


def in_vmem():
    return pl.BlockSpec(memory_space=pltpu.VMEM)


def in_place():
    return pl.BlockSpec(memory_space=pltpu.HBM)


def kept_in_hbm(value):
    return pltpu.with_memory_space_constraint(value, pltpu.HBM)


def own_terms(counts, pairs, ranks, amps, panels):
    owned, width, _ = amps.shape
    orbitals, slots, _, _ = panels.shape
    paired = (orbitals, slots // 2, SLAB, WIDE)
    return pl.pallas_call(
        own_body,
        out_shape=(
            jax.ShapeDtypeStruct((2, owned, width // 2, width), F32),
            pltpu.VMEM(paired, BF16),
        ),
        in_specs=[in_place(), in_place(), in_place(), in_vmem(), in_place()],
        out_specs=(in_vmem(), in_vmem()),
        scratch_shapes=[
            pltpu.VMEM(panels.shape, BF16),
            pltpu.VMEM((WIDE, WIDE), BF16),
            pltpu.SMEM(counts.shape, jnp.int32),
            pltpu.SMEM(pairs.shape, jnp.int32),
            pltpu.SMEM(ranks.shape, jnp.int32),
            pltpu.SemaphoreType.DMA((orbitals,)),
            pltpu.SemaphoreType.DMA((3,)),
        ],
        cost_estimate=pl.CostEstimate(flops=4 * 10**9, bytes_accessed=5 * 10**6, transcendentals=0),
        compiler_params=pltpu.CompilerParams(vmem_limit_bytes=16 * 2**20),
        name="own_terms",
    )(counts, pairs, ranks, amps, panels)


def other_terms(pairs, ranks, near, far, paired):
    owned, width, _ = near.shape
    shape = jax.ShapeDtypeStruct((2, owned, width // 2, width), BF16)
    return pl.pallas_call(
        other_body,
        out_shape=(shape, shape),
        in_specs=[in_place(), in_place(), in_vmem(), in_vmem(), in_vmem()],
        out_specs=(in_vmem(), in_vmem()),
        scratch_shapes=[
            pltpu.VMEM((WIDE, WIDE), BF16),
            pltpu.SMEM(pairs.shape, jnp.int32),
            pltpu.SMEM(ranks.shape, jnp.int32),
            pltpu.SemaphoreType.DMA((2,)),
        ],
        cost_estimate=pl.CostEstimate(flops=8 * 10**9, bytes_accessed=5 * 10**6, transcendentals=0),
        compiler_params=pltpu.CompilerParams(vmem_limit_bytes=16 * 2**20),
        name="other_terms",
    )(pairs, ranks, near, far, paired)


def passed_along(value, axis, steps):
    count = lax.axis_size(axis)
    return lax.ppermute(value, axis, [(source, (source + steps) % count) for source in range(count)])


def shards(panels, aux_counts, pair_list, pair_ranks, amplitudes):
    side = lax.axis_index("aux")
    panels = kept_in_hbm(panels)
    pairs = kept_in_hbm(pair_list.T)
    pair_ranks = kept_in_hbm(pair_ranks)
    aux_counts = kept_in_hbm(aux_counts)
    far_amps = passed_along(amplitudes, "blk", -2)
    near_amps = passed_along(amplitudes, "blk", -1)
    own, paired = own_terms(aux_counts, pairs, pair_ranks, amplitudes, panels)
    near, far = other_terms(pairs, pair_ranks, near_amps, far_amps, paired)
    far = passed_along(far, "blk", 2)
    near = passed_along(near, "blk", 1)

    def summed(which):
        parts = [lax.dynamic_index_in_dim(x, which, 0, keepdims=False).astype(F32) for x in (own, near, far)]
        return parts[0] + parts[1] + parts[2]

    received = passed_along(summed(1 - side).astype(BF16), "aux", 1)
    return summed(side) + received.astype(F32)


def solution(mesh):
    placed = (P(None, ("blk", "aux"), None, None), P(), P(), P(), P("blk", None, None))
    return jax.shard_map(
        shards, mesh=mesh, in_specs=placed, out_specs=P("blk", "aux", None), check_vma=False
    )
```

time: 142 us -> 45.1 us (0.32)
  loops' own time: 45.1 us -> 0 us
  matrix products: 39.7 us -> 0 us
  Pallas kernels: 0 us -> 16.9 us
  local copies, waits for them, and re-layouts: 18.3 us -> 1.63 us
  other arithmetic: 16 us -> 0.06 us
  waiting for transfers between devices: 0.01 us -> 12.4 us
  blocking collectives: 9.42 us -> 0 us
  starting transfers between devices: 12 us -> 14.1 us
    another operation x3 -> x0, loops' own time: 45.1 us -> none  [ladder(): return lax.map(one_pair, (pair_rows, rank_rows, amp_rows))]
    dot_general x12 -> x0, matrix products: 39.7 us -> none  [one_pair(): jnp.einsum('sad,sbd->ab', half_step, right_panel, preferred_element_type=...]
    pallas_call x0 -> x2, Pallas kernels: none -> 16.9 us  [the longest x1 9.51 us: other_terms(): pl.pallas_call(other_body, out_shape=(shape, shape), in_specs=[in_place()...]
    lt x24 -> x0, other arithmetic: 15.2 us -> none  [the longest x12 7.64 us: one_pair(): kept_mask = positions < rank_value]
    ppermute x4 -> x5, waiting for transfers between devices: 0.01 us -> 12.4 us  [passed_along(): lax.ppermute(value, axis, [(source, (source + steps) % count) for source...]
    dynamic_slice x27 -> x0, local copies, waits for them, and re-layouts: 11.3 us -> none  [the longest x24 8.3 us: ladder(): return lax.map(one_pair, (pair_rows, rank_rows, amp_rows))]
    all_to_all x1 -> x0, blocking collectives: 9.42 us -> none  [sent_and_summed(): lax.all_to_all(in_blocks(shard, dim, devices), axis, 0, 0, tiled=True)]
    slice x12 -> x0, local copies, waits for them, and re-layouts: 6.82 us -> none  [one_pair(): left_panel = lax.dynamic_index_in_dim(block, orbitals[0], 0, keepdims=False)]
  transfers between devices with their start and end apart: 4 -> 5, of which waited for: 0 -> 3; matrix products, arithmetic and copies ran while one was open for 52% -> 0% of each run, Pallas kernels for 0% -> 16%
where the time goes in v1:
time: 45.1 us; the launch traced here: 45 us
  Pallas kernels  16.9 us (37%)
  starting transfers between devices  14.1 us (31%)
  waiting for transfers between devices  12.4 us (27%)
  local copies, waits for them, and re-layouts  1.63 us (4%)
    ppermute x5, starting transfers between devices, passed_along(): lax.ppermute(value, axis, [(source, (source + steps) % count) for source...  14.1 us
    ppermute x5, waiting for transfers between devices, passed_along(): lax.ppermute(value, axis, [(source, (source + steps) % count) for source...  12.4 us
    pallas_call x1, Pallas kernels, other_terms(): pl.pallas_call(other_body, out_shape=(shape, shape), in_specs=[in_place()...  9.51 us
    pallas_call x1, Pallas kernels, own_terms(): pl.pallas_call(own_body, out_shape=(jax.ShapeDtypeStruct((2, owned, width...  7.34 us
  transfers between devices with their start and end apart: 5, of which 3 were waited for; matrix products, arithmetic and copies ran while one was open for 0% of the time, Pallas kernels for 16%

profile of v1, /device:TPU:1, one launch (start us, length us, event | category | flops | bytes accessed | tf_op | source)
XLA Modules:
  0.0 45.0 jit_solution(7933189229731990680)
XLA Ops:
  0.0 9.8 %collective-permute-start.1 = (bf16[4,120,120]{2,1,0:T(8,128)(2,1)}, bf16[4,120,120]{2,1,0:T(8,128)(2,1)S(1)}, u32[]{:S(2)}, u32[]{:S(2)}) collective-permute-start(bf16[4,120,120]{2,1,0:T(8,128)(2,1)} %amps.1), channel_id=1, source_target_pairs={{0,252},{2,254},{4,0},{6,2},{8,4},{10,6},{12,8},{14,10},{16,12},{1... | collective-permute-start | bytes 345608 | tf_op jit(solution)/shard_map/ppermute | solution.py:175
  9.8 1.0 %collective-permute-start = (bf16[4,120,120]{2,1,0:T(8,128)(2,1)}, bf16[4,120,120]{2,1,0:T(8,128)(2,1)S(1)}, u32[]{:S(2)}, u32[]{:S(2)}) collective-permute-start(bf16[4,120,120]{2,1,0:T(8,128)(2,1)} %amps.1), channel_id=1, source_target_pairs={{0,254},{2,0},{4,2},{6,4},{8,6},{10,8},{12,10},{14,12},{16,14},{18... | collective-permute-start | bytes 345608 | tf_op jit(solution)/shard_map/ppermute | solution.py:175
  10.7 0.0 copy-start
  10.7 0.9 %copy-done = bf16[4,120,120]{2,1,0:T(8,128)(2,1)S(1)} copy-done((bf16[4,120,120]{2,1,0:T(8,128)(2,1)S(1)}, bf16[4,120,120]{2,1,0:T(8,128)(2,1)}, u32[]{:S(2)}) %copy-start) | copy-done | bytes 115224
  11.6 7.3 %own_terms.1 = (f32[2,4,60,120]{3,2,1,0:T(8,128)S(1)}, bf16[4,22,128,256]{3,2,1,0:T(8,128)(2,1)S(1)}) custom-call(s32[256]{0:T(256)} %counts.1, s32[2,512]{1,0:T(2,128)} %bitcast.5, s32[512]{0:T(512)} %ranks.3, bf16[4,120,120]{2,1,0:T(8,128)(2,1)S(1)} %copy-done, bf16[4,44,120,120]{3,2,1,0:T(8,128)(2,1)} %panels.1), custom_call_target="tpu_custom_call" | custom-call | flops 4000000000 | bytes 5000000 | tf_op jit(solution)/shard_map/own_terms/pallas_call | solution.py:130
  19.0 0.0 collective-permute-done.1.far
  19.0 0.0 collective-permute-done.near
  19.0 9.5 %other_terms.1 = (bf16[2,4,60,120]{3,2,1,0:T(8,128)(2,1)S(1)}, bf16[2,4,60,120]{3,2,1,0:T(8,128)(2,1)S(1)}) custom-call(s32[2,512]{1,0:T(2,128)} %bitcast.6, s32[512]{0:T(512)} %ranks.3, bf16[4,120,120]{2,1,0:T(8,128)(2,1)S(1)} %collective-permute-done.near, bf16[4,120,120]{2,1,0:T(8,128)(2,1)S(1)} %collective-permute-done.1.far, ...), custom_call_target="tpu_custom_call" | custom-call | flops 8000000000 | bytes 5000000 | tf_op jit(solution)/shard_map/other_terms/pallas_call | solution.py:156
  28.5 0.9 %collective-permute-start.2 = (bf16[2,4,60,120]{3,2,1,0:T(8,128)(2,1)S(1)}, bf16[2,4,60,120]{3,2,1,0:T(8,128)(2,1)S(1)}, u32[]{:S(2)}, u32[]{:S(2)}) collective-permute-start(bf16[2,4,60,120]{3,2,1,0:T(8,128)(2,1)S(1)} %get-tuple-element.11), channel_id=1, source_target_pairs={{0,2},{2,4},{4,6},{6,8},{8,10},{10,12},{12,14},{14,16},{16,18},{18... | collective-permute-start | bytes 345608 | tf_op jit(solution)/shard_map/ppermute | solution.py:175
  29.4 0.0 collective-permute-start.3
  29.4 2.6 %collective-permute-done.2 = bf16[2,4,60,120]{3,2,1,0:T(8,128)(2,1)S(1)} collective-permute-done((bf16[2,4,60,120]{3,2,1,0:T(8,128)(2,1)S(1)}, bf16[2,4,60,120]{3,2,1,0:T(8,128)(2,1)S(1)}, u32[]{:S(2)}, u32[]{:S(2)}) %collective-permute-start.2) | collective-permute-done | bytes 115232 | tf_op jit(solution)/shard_map/ppermute | solution.py:175
  32.1 7.4 %collective-permute-done.3 = bf16[2,4,60,120]{3,2,1,0:T(8,128)(2,1)S(1)} collective-permute-done((bf16[2,4,60,120]{3,2,1,0:T(8,128)(2,1)S(1)}, bf16[2,4,60,120]{3,2,1,0:T(8,128)(2,1)S(1)}, u32[]{:S(2)}, u32[]{:S(2)}) %collective-permute-start.3) | collective-permute-done | bytes 115232 | tf_op jit(solution)/shard_map/ppermute | solution.py:175
  39.5 2.4 %collective-permute-start.4 = (bf16[4,60,120]{2,1,0:T(8,128)(2,1)S(1)}, bf16[4,60,120]{2,1,0:T(8,128)(2,1)S(1)}, u32[]{:S(2)}, u32[]{:S(2)}) collective-permute-start(bf16[4,60,120]{2,1,0:T(8,128)(2,1)S(1)} %fusion), channel_id=1, source_target_pairs={{0,1},{1,0},{2,3},{3,2},{4,5},{5,4},{6,7},{7,6},{8,9},{9,8},{10,11... | collective-permute-start | bytes 172808 | tf_op jit(solution)/shard_map/ppermute | solution.py:175
  42.0 2.3 %collective-permute-done.4 = bf16[4,60,120]{2,1,0:T(8,128)(2,1)S(1)} collective-permute-done((bf16[4,60,120]{2,1,0:T(8,128)(2,1)S(1)}, bf16[4,60,120]{2,1,0:T(8,128)(2,1)S(1)}, u32[]{:S(2)}, u32[]{:S(2)}) %collective-permute-start.4) | collective-permute-done | bytes 57632 | tf_op jit(solution)/shard_map/ppermute | solution.py:175
  44.3 0.7 %copy.6 = f32[4,60,120]{2,0,1:T(4,128)} copy(f32[4,60,120]{2,1,0:T(8,128)S(1)} %bitcast_add_fusion) | data formatting | bytes 230400 | tf_op jit(solution)/shard_map/add | solution.py:196
  (2 shorter events, 0.1 us)
Async XLA Ops:
  0.0 19.0 %collective-permute-start.1 = (bf16[4,120,120]{2,1,0:T(8,128)(2,1)}, bf16[4,120,120]{2,1,0:T(8,128)(2,1)S(1)}, u32[]{:S(2)}, u32[]{:S(2)}) collective-permute-start(bf16[4,120,120]{2,1,0:T(8,128)(2,1)} %amps.1), channel_id=1, source_target_pairs={{0,252},{2,254},{4,0},{6,2},{8,4},{10,6},{12,8},{14,10},{16,12},{1... | collective-permute-start | bytes 345608 | tf_op jit(solution)/shard_map/ppermute | solution.py:175
  9.8 9.2 %collective-permute-start = (bf16[4,120,120]{2,1,0:T(8,128)(2,1)}, bf16[4,120,120]{2,1,0:T(8,128)(2,1)S(1)}, u32[]{:S(2)}, u32[]{:S(2)}) collective-permute-start(bf16[4,120,120]{2,1,0:T(8,128)(2,1)} %amps.1), channel_id=1, source_target_pairs={{0,254},{2,0},{4,2},{6,4},{8,6},{10,8},{12,10},{14,12},{16,14},{18... | collective-permute-start | bytes 345608 | tf_op jit(solution)/shard_map/ppermute | solution.py:175
  10.7 0.9 %copy-start = (bf16[4,120,120]{2,1,0:T(8,128)(2,1)S(1)}, bf16[4,120,120]{2,1,0:T(8,128)(2,1)}, u32[]{:S(2)}) copy-start(bf16[4,120,120]{2,1,0:T(8,128)(2,1)} %amps.1) | copy-start | bytes 345604
  28.5 3.5 %collective-permute-start.2 = (bf16[2,4,60,120]{3,2,1,0:T(8,128)(2,1)S(1)}, bf16[2,4,60,120]{3,2,1,0:T(8,128)(2,1)S(1)}, u32[]{:S(2)}, u32[]{:S(2)}) collective-permute-start(bf16[2,4,60,120]{3,2,1,0:T(8,128)(2,1)S(1)} %get-tuple-element.11), channel_id=1, source_target_pairs={{0,2},{2,4},{4,6},{6,8},{8,10},{10,12},{12,14},{14,16},{16,18},{18... | collective-permute-start | bytes 345608 | tf_op jit(solution)/shard_map/ppermute | solution.py:175
  29.4 10.1 %collective-permute-start.3 = (bf16[2,4,60,120]{3,2,1,0:T(8,128)(2,1)S(1)}, bf16[2,4,60,120]{3,2,1,0:T(8,128)(2,1)S(1)}, u32[]{:S(2)}, u32[]{:S(2)}) collective-permute-start(bf16[2,4,60,120]{3,2,1,0:T(8,128)(2,1)S(1)} %get-tuple-element.12), channel_id=1, source_target_pairs={{0,4},{2,6},{4,8},{6,10},{8,12},{10,14},{12,16},{14,18},{16,20},{1... | collective-permute-start | bytes 345608 | tf_op jit(solution)/shard_map/ppermute | solution.py:175
  39.5 4.7 %collective-permute-start.4 = (bf16[4,60,120]{2,1,0:T(8,128)(2,1)S(1)}, bf16[4,60,120]{2,1,0:T(8,128)(2,1)S(1)}, u32[]{:S(2)}, u32[]{:S(2)}) collective-permute-start(bf16[4,60,120]{2,1,0:T(8,128)(2,1)S(1)} %fusion), channel_id=1, source_target_pairs={{0,1},{1,0},{2,3},{3,2},{4,5},{5,4},{6,7},{7,6},{8,9},{9,8},{10,11... | collective-permute-start | bytes 172808 | tf_op jit(solution)/shard_map/ppermute | solution.py:175

commit v2 on v1

v2 whole, which is shorter than its diff:
```python
import functools
import jax
import jax.numpy as jnp
from jax import lax
from jax.experimental import pallas as pl
from jax.experimental.pallas import tpu as pltpu
from jax.sharding import PartitionSpec as P

F32, BF16 = jnp.float32, jnp.bfloat16
SLAB = 128
WIDE = 256
STEP = 2


def table_copies(pairs, ranks, pairs_s, ranks_s, sems):
    return [
        pltpu.make_async_copy(pairs, pairs_s, sems.at[0]),
        pltpu.make_async_copy(ranks, ranks_s, sems.at[1]),
    ]


def one_pair(row, amps, put, paired, both, pairs_s, ranks_s, width):
    left, right, rank = pairs_s[0, row], pairs_s[1, row], ranks_s[row]
    rows = lax.broadcasted_iota(jnp.int32, (width, width), 0)
    cols = lax.broadcasted_iota(jnp.int32, (width, width), 1)
    keep = (rows < rank) & (cols < rank)
    masked = jnp.where(keep, amps, jnp.zeros_like(amps))
    both[0:width, 0:width] = masked
    both[SLAB : SLAB + width, SLAB : SLAB + width] = masked
    total = jnp.zeros((SLAB, SLAB), F32)
    slot_pairs = paired.shape[1]
    for first in range(0, slot_pairs, STEP):
        taken = min(STEP, slot_pairs - first)
        lhs = paired[left, first : first + taken].reshape(taken * SLAB, WIDE)
        half = jnp.dot(lhs, both[...], preferred_element_type=F32)
        for k in range(taken):
            part = half[k * SLAB : (k + 1) * SLAB].astype(BF16)
            total = total + lax.dot_general(
                part, paired[right, first + k], (((1,), (1,)), ((), ())), preferred_element_type=F32
            )
    put(jnp.where(keep, total[:width, :width], 0.0))


def load_body(counts, panels, paired, raw, counts_s, sems, count_sem):
    orbitals, slots, width, _ = panels.shape
    shard = lax.axis_index("blk") * lax.axis_size("aux") + lax.axis_index("aux")
    copies = [pltpu.make_async_copy(panels.at[o], raw.at[o], sems.at[o]) for o in range(orbitals)]
    small = pltpu.make_async_copy(counts, counts_s, count_sem)
    small.start()
    for copy in copies:
        copy.start()
    small.wait()
    live = counts_s[shard]
    for o in range(orbitals):
        copies[o].wait()

        def widen(t, carry):
            for side in range(2):
                slot = 2 * t + side
                slab = raw[o, slot]
                slab = jnp.where(slot < live, slab, jnp.zeros_like(slab))
                slab = jnp.pad(slab, ((0, SLAB - width), (0, SLAB - width)))
                paired[o, t, :, side * SLAB : (side + 1) * SLAB] = slab
            return carry

        lax.fori_loop(0, slots // 2, widen, 0, unroll=2)


def group(first, amps, out, paired, both, pairs_s, ranks_s):
    owned, width, _ = amps.shape
    cut = width // 2

    def pair(p, carry):
        def put(value):
            out[0, p] = value[:cut].astype(out.dtype)
            out[1, p] = value[cut:].astype(out.dtype)

        one_pair(first + p, amps[p], put, paired, both, pairs_s, ranks_s, width)
        return carry

    lax.fori_loop(0, owned, pair, 0)


def own_body(pairs, ranks, amps, paired, after, out, both, pairs_s, ranks_s, sems):
    del after
    small = table_copies(pairs, ranks, pairs_s, ranks_s, sems)
    for copy in small:
        copy.start()
    both[...] = jnp.zeros_like(both)
    for copy in small:
        copy.wait()
    group(lax.axis_index("blk") * amps.shape[0], amps, out, paired, both, pairs_s, ranks_s)


def other_body(pairs, ranks, near, far, paired, near_out, far_out, both, pairs_s, ranks_s, sems):
    owned = near.shape[0]
    blocks = lax.axis_size("blk")
    block = lax.axis_index("blk")
    small = table_copies(pairs, ranks, pairs_s, ranks_s, sems)
    for copy in small:
        copy.start()
    both[...] = jnp.zeros_like(both)
    for copy in small:
        copy.wait()
    for amps, out, hops in ((far, far_out, 2), (near, near_out, 1)):
        group((block + hops) % blocks * owned, amps, out, paired, both, pairs_s, ranks_s)


def in_vmem():
    return pl.BlockSpec(memory_space=pltpu.VMEM)


def in_place():
    return pl.BlockSpec(memory_space=pltpu.HBM)


def kept_in_hbm(value):
    return pltpu.with_memory_space_constraint(value, pltpu.HBM)


def loaded(counts, panels):
    orbitals, slots, _, _ = panels.shape
    return pl.pallas_call(
        load_body,
        out_shape=pltpu.VMEM((orbitals, slots // 2, SLAB, WIDE), BF16),
        in_specs=[in_place(), in_place()],
        out_specs=in_vmem(),
        scratch_shapes=[
            pltpu.VMEM(panels.shape, BF16),
            pltpu.SMEM(counts.shape, jnp.int32),
            pltpu.SemaphoreType.DMA((orbitals,)),
            pltpu.SemaphoreType.DMA(()),
        ],
        cost_estimate=pl.CostEstimate(flops=10**9, bytes_accessed=5 * 10**6, transcendentals=0),
        compiler_params=pltpu.CompilerParams(vmem_limit_bytes=16 * 2**20),
        name="loaded",
    )(counts, panels)


def table_scratch(pairs, ranks):
    return [
        pltpu.VMEM((WIDE, WIDE), BF16),
        pltpu.SMEM(pairs.shape, jnp.int32),
        pltpu.SMEM(ranks.shape, jnp.int32),
        pltpu.SemaphoreType.DMA((2,)),
    ]


def own_terms(pairs, ranks, amps, paired, after):
    owned, width, _ = amps.shape
    return pl.pallas_call(
        own_body,
        out_shape=jax.ShapeDtypeStruct((2, owned, width // 2, width), F32),
        in_specs=[in_place(), in_place(), in_vmem(), in_vmem(), pl.BlockSpec(memory_space=pl.ANY)],
        out_specs=in_vmem(),
        scratch_shapes=table_scratch(pairs, ranks),
        cost_estimate=pl.CostEstimate(flops=4 * 10**9, bytes_accessed=5 * 10**6, transcendentals=0),
        compiler_params=pltpu.CompilerParams(vmem_limit_bytes=8 * 2**20),
        name="own_terms",
    )(pairs, ranks, amps, paired, after)


def other_terms(pairs, ranks, near, far, paired):
    owned, width, _ = near.shape
    shape = jax.ShapeDtypeStruct((2, owned, width // 2, width), BF16)
    return pl.pallas_call(
        other_body,
        out_shape=(shape, shape),
        in_specs=[in_place(), in_place(), in_vmem(), in_vmem(), in_vmem()],
        out_specs=(in_vmem(), in_vmem()),
        scratch_shapes=table_scratch(pairs, ranks),
        cost_estimate=pl.CostEstimate(flops=8 * 10**9, bytes_accessed=5 * 10**6, transcendentals=0),
        compiler_params=pltpu.CompilerParams(vmem_limit_bytes=8 * 2**20),
        name="other_terms",
    )(pairs, ranks, near, far, paired)


def passed_along(value, axis, steps):
    count = lax.axis_size(axis)
    return lax.ppermute(value, axis, [(source, (source + steps) % count) for source in range(count)])


def shards(panels, aux_counts, pair_list, pair_ranks, amplitudes):
    side = lax.axis_index("aux")
    pairs = kept_in_hbm(pair_list.T)
    ranks = kept_in_hbm(pair_ranks)
    far_amps = passed_along(amplitudes, "blk", -2)
    near_amps = passed_along(amplitudes, "blk", -1)
    paired = loaded(kept_in_hbm(aux_counts), kept_in_hbm(panels))
    near, far = other_terms(pairs, ranks, near_amps, far_amps, paired)
    own = own_terms(pairs, ranks, amplitudes, paired, far)
    far = passed_along(far, "blk", 2)
    near = passed_along(near, "blk", 1)

    def summed(which):
        parts = [lax.dynamic_index_in_dim(x, which, 0, keepdims=False).astype(F32) for x in (own, near, far)]
        return parts[0] + parts[1] + parts[2]

    received = passed_along(summed(1 - side).astype(BF16), "aux", 1)
    return summed(side) + received.astype(F32)


def solution(mesh):
    placed = (P(None, ("blk", "aux"), None, None), P(), P(), P(), P("blk", None, None))
    return jax.shard_map(
        shards, mesh=mesh, in_specs=placed, out_specs=P("blk", "aux", None), check_vma=False
    )
```

time: 45.1 us -> 40.9 us (0.907)
  the two profiles are of different devices: /device:TPU:1 before, /device:TPU:4 now
where the time goes in v2:
time: 40.9 us; the launch traced here: 40.7 us
  Pallas kernels  17.7 us (43%)
  waiting for transfers between devices  12 us (29%)
  starting transfers between devices  10.2 us (25%)
  local copies, waits for them, and re-layouts  0.73 us (2%)
    ppermute x5, waiting for transfers between devices, passed_along(): lax.ppermute(value, axis, [(source, (source + steps) % count) for source...  12 us
    ppermute x5, starting transfers between devices, passed_along(): lax.ppermute(value, axis, [(source, (source + steps) % count) for source...  10.2 us
    pallas_call x1, Pallas kernels, other_terms(): pl.pallas_call(other_body, out_shape=(shape, shape), in_specs=[in_place()...  9.6 us
    pallas_call x1, Pallas kernels, own_terms(): pl.pallas_call(own_body, out_shape=jax.ShapeDtypeStruct((2, owned, width...  5.1 us
    pallas_call x1, Pallas kernels, loaded(): pl.pallas_call(load_body, out_shape=pltpu.VMEM((orbitals, slots // 2, SLA...  2.98 us
  transfers between devices with their start and end apart: 5, of which 4 were waited for; matrix products, arithmetic and copies ran while one was open for 0% of the time, Pallas kernels for 20%

profile of v2, /device:TPU:4, one launch (start us, length us, event | category | flops | bytes accessed | tf_op | source)
XLA Modules:
  0.0 40.7 jit_solution(10509542808039923022)
XLA Ops:
  0.0 8.4 %collective-permute-start = (bf16[4,120,120]{2,1,0:T(8,128)(2,1)}, bf16[4,120,120]{2,1,0:T(8,128)(2,1)S(1)}, u32[]{:S(2)}, u32[]{:S(2)}) collective-permute-start(bf16[4,120,120]{2,1,0:T(8,128)(2,1)} %amps.1), channel_id=1, source_target_pairs={{0,254},{2,0},{4,2},{6,4},{8,6},{10,8},{12,10},{14,12},{16,14},{18... | collective-permute-start | bytes 345608 | tf_op jit(solution)/shard_map/ppermute | solution.py:180
  8.4 0.7 %collective-permute-start.1 = (bf16[4,120,120]{2,1,0:T(8,128)(2,1)}, bf16[4,120,120]{2,1,0:T(8,128)(2,1)S(1)}, u32[]{:S(2)}, u32[]{:S(2)}) collective-permute-start(bf16[4,120,120]{2,1,0:T(8,128)(2,1)} %amps.1), channel_id=1, source_target_pairs={{0,252},{2,254},{4,0},{6,2},{8,4},{10,6},{12,8},{14,10},{16,12},{1... | collective-permute-start | bytes 345608 | tf_op jit(solution)/shard_map/ppermute | solution.py:180
  9.1 3.0 %loaded.1.paired = bf16[4,22,128,256]{3,2,1,0:T(8,128)(2,1)S(1)} custom-call(s32[256]{0:T(256)} %counts.1, bf16[4,44,120,120]{3,2,1,0:T(8,128)(2,1)} %panels.1), custom_call_target="tpu_custom_call" | custom-call | flops 1000000000 | bytes 5000000 | tf_op jit(solution)/shard_map/loaded/pallas_call | solution.py:123
  12.1 0.2 collective-permute-done.near
  12.3 1.4 %collective-permute-done.1.far = bf16[4,120,120]{2,1,0:T(8,128)(2,1)S(1)} collective-permute-done((bf16[4,120,120]{2,1,0:T(8,128)(2,1)}, bf16[4,120,120]{2,1,0:T(8,128)(2,1)S(1)}, u32[]{:S(2)}, u32[]{:S(2)}) %collective-permute-start.1) | collective-permute-done | bytes 115232 | tf_op jit(solution)/shard_map/ppermute | solution.py:180
  13.7 0.0 copy-start
  13.7 9.6 %other_terms.1 = (bf16[2,4,60,120]{3,2,1,0:T(8,128)(2,1)S(1)}, bf16[2,4,60,120]{3,2,1,0:T(8,128)(2,1)S(1)}) custom-call(s32[2,512]{1,0:T(2,128)} %bitcast.5, s32[512]{0:T(512)} %ranks.3, bf16[4,120,120]{2,1,0:T(8,128)(2,1)S(1)} %collective-permute-done.near, bf16[4,120,120]{2,1,0:T(8,128)(2,1)S(1)} %collective-permute-done.1.far, ...), custom_call_target="tpu_custom_call" | custom-call | flops 8000000000 | bytes 5000000 | tf_op jit(solution)/shard_map/other_terms/pallas_call | solution.py:166
  23.3 0.1 collective-permute-start.3
  23.4 0.1 collective-permute-start.2
  23.5 0.0 copy-done
  23.5 5.1 %own_terms.1 = f32[2,4,60,120]{3,2,1,0:T(8,128)S(1)} custom-call(s32[2,512]{1,0:T(2,128)} %bitcast.6, s32[512]{0:T(512)} %ranks.3, bf16[4,120,120]{2,1,0:T(8,128)(2,1)S(1)} %copy-done, bf16[4,22,128,256]{3,2,1,0:T(8,128)(2,1)S(1)} %loaded.1.paired, bf16[2,4,60,120]{3,2,1,0:T(8,128)(2,1)S(1)} %get-tuple-element.7.after), custom_call_target="tpu_custom_call" | custom-call | flops 4000000000 | bytes 5000000 | tf_op jit(solution)/shard_map/own_terms/pallas_call | solution.py:151
  28.6 5.4 %collective-permute-done.3 = bf16[2,4,60,120]{3,2,1,0:T(8,128)(2,1)S(1)} collective-permute-done((bf16[2,4,60,120]{3,2,1,0:T(8,128)(2,1)S(1)}, bf16[2,4,60,120]{3,2,1,0:T(8,128)(2,1)S(1)}, u32[]{:S(2)}, u32[]{:S(2)}) %collective-permute-start.3) | collective-permute-done | bytes 115232 | tf_op jit(solution)/shard_map/ppermute | solution.py:180
  34.1 0.0 collective-permute-done.2
  34.1 0.9 %collective-permute-start.4 = (bf16[4,60,120]{2,1,0:T(8,128)(2,1)S(1)}, bf16[4,60,120]{2,1,0:T(8,128)(2,1)S(1)}, u32[]{:S(2)}, u32[]{:S(2)}) collective-permute-start(bf16[4,60,120]{2,1,0:T(8,128)(2,1)S(1)} %fusion), channel_id=1, source_target_pairs={{0,1},{1,0},{2,3},{3,2},{4,5},{5,4},{6,7},{7,6},{8,9},{9,8},{10,11... | collective-permute-start | bytes 172808 | tf_op jit(solution)/shard_map/ppermute | solution.py:180
  35.0 5.0 %collective-permute-done.4 = bf16[4,60,120]{2,1,0:T(8,128)(2,1)S(1)} collective-permute-done((bf16[4,60,120]{2,1,0:T(8,128)(2,1)S(1)}, bf16[4,60,120]{2,1,0:T(8,128)(2,1)S(1)}, u32[]{:S(2)}, u32[]{:S(2)}) %collective-permute-start.4) | collective-permute-done | bytes 57632 | tf_op jit(solution)/shard_map/ppermute | solution.py:180
  40.0 0.7 %copy.6 = f32[4,60,120]{2,0,1:T(4,128)} copy(f32[4,60,120]{2,1,0:T(8,128)S(1)} %bitcast_add_fusion) | data formatting | bytes 230400 | tf_op jit(solution)/shard_map/add | solution.py:200
  (2 shorter events, 0.1 us)
Async XLA Ops:
  0.0 12.3 %collective-permute-start = (bf16[4,120,120]{2,1,0:T(8,128)(2,1)}, bf16[4,120,120]{2,1,0:T(8,128)(2,1)S(1)}, u32[]{:S(2)}, u32[]{:S(2)}) collective-permute-start(bf16[4,120,120]{2,1,0:T(8,128)(2,1)} %amps.1), channel_id=1, source_target_pairs={{0,254},{2,0},{4,2},{6,4},{8,6},{10,8},{12,10},{14,12},{16,14},{18... | collective-permute-start | bytes 345608 | tf_op jit(solution)/shard_map/ppermute | solution.py:180
  8.4 5.3 %collective-permute-start.1 = (bf16[4,120,120]{2,1,0:T(8,128)(2,1)}, bf16[4,120,120]{2,1,0:T(8,128)(2,1)S(1)}, u32[]{:S(2)}, u32[]{:S(2)}) collective-permute-start(bf16[4,120,120]{2,1,0:T(8,128)(2,1)} %amps.1), channel_id=1, source_target_pairs={{0,252},{2,254},{4,0},{6,2},{8,4},{10,6},{12,8},{14,10},{16,12},{1... | collective-permute-start | bytes 345608 | tf_op jit(solution)/shard_map/ppermute | solution.py:180
  13.7 9.8 %copy-start = (bf16[4,120,120]{2,1,0:T(8,128)(2,1)S(1)}, bf16[4,120,120]{2,1,0:T(8,128)(2,1)}, u32[]{:S(2)}) copy-start(bf16[4,120,120]{2,1,0:T(8,128)(2,1)} %amps.1) | copy-start | bytes 345604
  23.3 10.7 %collective-permute-start.3 = (bf16[2,4,60,120]{3,2,1,0:T(8,128)(2,1)S(1)}, bf16[2,4,60,120]{3,2,1,0:T(8,128)(2,1)S(1)}, u32[]{:S(2)}, u32[]{:S(2)}) collective-permute-start(bf16[2,4,60,120]{3,2,1,0:T(8,128)(2,1)S(1)} %get-tuple-element.7.after), channel_id=1, source_target_pairs={{0,4},{2,6},{4,8},{6,10},{8,12},{10,14},{12,16},{14,18},{16,20},{1... | collective-permute-start | bytes 345608 | tf_op jit(solution)/shard_map/ppermute | solution.py:180
  23.4 10.6 %collective-permute-start.2 = (bf16[2,4,60,120]{3,2,1,0:T(8,128)(2,1)S(1)}, bf16[2,4,60,120]{3,2,1,0:T(8,128)(2,1)S(1)}, u32[]{:S(2)}, u32[]{:S(2)}) collective-permute-start(bf16[2,4,60,120]{3,2,1,0:T(8,128)(2,1)S(1)} %get-tuple-element.8), channel_id=1, source_target_pairs={{0,2},{2,4},{4,6},{6,8},{8,10},{10,12},{12,14},{14,16},{16,18},{18... | collective-permute-start | bytes 345608 | tf_op jit(solution)/shard_map/ppermute | solution.py:180
  34.1 5.9 %collective-permute-start.4 = (bf16[4,60,120]{2,1,0:T(8,128)(2,1)S(1)}, bf16[4,60,120]{2,1,0:T(8,128)(2,1)S(1)}, u32[]{:S(2)}, u32[]{:S(2)}) collective-permute-start(bf16[4,60,120]{2,1,0:T(8,128)(2,1)S(1)} %fusion), channel_id=1, source_target_pairs={{0,1},{1,0},{2,3},{3,2},{4,5},{5,4},{6,7},{7,6},{8,9},{9,8},{10,11... | collective-permute-start | bytes 172808 | tf_op jit(solution)/shard_map/ppermute | solution.py:180

commit v3 on v2

v3 whole, which is shorter than its diff:
```python
import jax
import jax.numpy as jnp
from jax import lax
from jax.experimental import pallas as pl
from jax.experimental.pallas import tpu as pltpu
from jax.sharding import PartitionSpec as P

F32, BF16 = jnp.float32, jnp.bfloat16
SLAB = 128
STEP = 2
EARLY = 2


def table_copies(pairs, ranks, pairs_s, ranks_s, sems):
    return [
        pltpu.make_async_copy(pairs, pairs_s, sems.at[0]),
        pltpu.make_async_copy(ranks, ranks_s, sems.at[1]),
    ]


def slot_pair(paired, orbital, t):
    return jnp.concatenate([paired[orbital, t, 0], paired[orbital, t, 1]], axis=1)


def on_diagonal(square):
    empty = jnp.zeros_like(square)
    upper = jnp.concatenate([square, empty], axis=1)
    lower = jnp.concatenate([empty, square], axis=1)
    return jnp.concatenate([upper, lower], axis=0)


def terms(work, paired, squares, pairs_s, ranks_s):
    slot_pairs = paired.shape[1]
    prepared = []
    for n, (row, amps, put) in enumerate(work):
        width = amps.shape[0]
        rank = ranks_s[row]
        rows = lax.broadcasted_iota(jnp.int32, (width, width), 0)
        cols = lax.broadcasted_iota(jnp.int32, (width, width), 1)
        masked = jnp.where((rows < rank) & (cols < rank), amps, jnp.zeros_like(amps))
        squares[n] = jnp.pad(masked, ((0, SLAB - width), (0, SLAB - width)))
        prepared.append((pairs_s[0, row], pairs_s[1, row], rank, rows, cols, put))
    for n, (left, right, rank, rows, cols, put) in enumerate(prepared):
        width = rows.shape[0]
        total = jnp.zeros((SLAB, SLAB), F32)
        for first in range(0, slot_pairs, STEP):
            taken = range(first, min(first + STEP, slot_pairs))
            lhs = jnp.concatenate([slot_pair(paired, left, t) for t in taken], axis=0)
            half = jnp.dot(lhs, on_diagonal(squares[n]), preferred_element_type=F32)
            for k, t in enumerate(taken):
                part = half[k * SLAB : (k + 1) * SLAB].astype(BF16)
                total = total + lax.dot_general(
                    part, slot_pair(paired, right, t), (((1,), (1,)), ((), ())), preferred_element_type=F32
                )
        put(jnp.where((rows < rank) & (cols < rank), total[:width, :width], 0.0))


def stored(out, p):
    def put(value):
        cut = value.shape[0] // 2
        out[0, p] = value[:cut].astype(out.dtype)
        out[1, p] = value[cut:].astype(out.dtype)

    return put


def load_body(counts, pairs, ranks, amps, panels, paired, out, raw, amps_v, squares, counts_s, pairs_s, ranks_s, sems, small_sems):
    orbitals, slots, width, _ = panels.shape
    owned = amps.shape[0]
    block = lax.axis_index("blk")
    shard = block * lax.axis_size("aux") + lax.axis_index("aux")
    small = table_copies(pairs, ranks, pairs_s, ranks_s, small_sems)
    small.append(pltpu.make_async_copy(counts, counts_s, small_sems.at[2]))
    small.append(pltpu.make_async_copy(amps.at[0:EARLY], amps_v, small_sems.at[3]))
    copies = [pltpu.make_async_copy(panels.at[o], raw.at[o], sems.at[o]) for o in range(orbitals)]
    for copy in small + copies:
        copy.start()
    for copy in small:
        copy.wait()
    live = counts_s[shard]
    for o in range(orbitals):
        copies[o].wait()

        def widen(t, carry):
            for side in range(2):
                slot = 2 * t + side
                slab = raw[o, slot]
                slab = jnp.where(slot < live, slab, jnp.zeros_like(slab))
                paired[o, t, side] = jnp.pad(slab, ((0, SLAB - width), (0, SLAB - width)))
            return carry

        lax.fori_loop(0, slots // 2, widen, 0, unroll=2)
    work = [(block * owned + p, amps_v[p], stored(out, p)) for p in range(EARLY)]
    terms(work, paired, squares, pairs_s, ranks_s)


def own_body(pairs, ranks, amps, paired, after, out, squares, pairs_s, ranks_s, sems):
    del after
    owned = amps.shape[0]
    small = table_copies(pairs, ranks, pairs_s, ranks_s, sems)
    for copy in small:
        copy.start()
    for copy in small:
        copy.wait()
    block = lax.axis_index("blk")
    work = [(block * owned + p, amps[p], stored(out, p - EARLY)) for p in range(EARLY, owned)]
    terms(work, paired, squares, pairs_s, ranks_s)


def other_body(pairs, ranks, near, far, paired, near_out, far_out, squares, pairs_s, ranks_s, sems):
    owned = near.shape[0]
    blocks = lax.axis_size("blk")
    block = lax.axis_index("blk")
    small = table_copies(pairs, ranks, pairs_s, ranks_s, sems)
    for copy in small:
        copy.start()
    for copy in small:
        copy.wait()
    work = []
    for amps, out, hops in ((far, far_out, 2), (near, near_out, 1)):
        start = (block + hops) % blocks * owned
        work += [(start + p, amps[p], stored(out, p)) for p in range(owned)]
    terms(work, paired, squares, pairs_s, ranks_s)


def in_vmem():
    return pl.BlockSpec(memory_space=pltpu.VMEM)


def in_place():
    return pl.BlockSpec(memory_space=pltpu.HBM)


def kept_in_hbm(value):
    return pltpu.with_memory_space_constraint(value, pltpu.HBM)


def cost(pairs):
    return pl.CostEstimate(flops=pairs * 10**9, bytes_accessed=5 * 10**6, transcendentals=0)


def halves(count, width, kind):
    return jax.ShapeDtypeStruct((2, count, width // 2, width), kind)


def loaded(counts, pairs, ranks, amps, panels):
    orbitals, slots, width, _ = panels.shape
    return pl.pallas_call(
        load_body,
        out_shape=(
            pltpu.VMEM((orbitals, slots // 2, 2, SLAB, SLAB), BF16),
            halves(EARLY, width, F32),
        ),
        in_specs=[in_place()] * 5,
        out_specs=(in_vmem(), in_vmem()),
        scratch_shapes=[
            pltpu.VMEM(panels.shape, BF16),
            pltpu.VMEM((EARLY, width, width), BF16),
            pltpu.VMEM((EARLY, SLAB, SLAB), BF16),
            pltpu.SMEM(counts.shape, jnp.int32),
            pltpu.SMEM(pairs.shape, jnp.int32),
            pltpu.SMEM(ranks.shape, jnp.int32),
            pltpu.SemaphoreType.DMA((orbitals,)),
            pltpu.SemaphoreType.DMA((4,)),
        ],
        cost_estimate=cost(3),
        compiler_params=pltpu.CompilerParams(vmem_limit_bytes=16 * 2**20),
        name="loaded",
    )(counts, pairs, ranks, amps, panels)


def table_scratch(count, pairs, ranks):
    return [
        pltpu.VMEM((count, SLAB, SLAB), BF16),
        pltpu.SMEM(pairs.shape, jnp.int32),
        pltpu.SMEM(ranks.shape, jnp.int32),
        pltpu.SemaphoreType.DMA((2,)),
    ]


def own_terms(pairs, ranks, amps, paired, after):
    owned, width, _ = amps.shape
    return pl.pallas_call(
        own_body,
        out_shape=halves(owned - EARLY, width, F32),
        in_specs=[in_place(), in_place(), in_vmem(), in_vmem(), pl.BlockSpec(memory_space=pl.ANY)],
        out_specs=in_vmem(),
        scratch_shapes=table_scratch(owned - EARLY, pairs, ranks),
        cost_estimate=cost(2 * owned),
        compiler_params=pltpu.CompilerParams(vmem_limit_bytes=8 * 2**20),
        name="own_terms",
    )(pairs, ranks, amps, paired, after)


def other_terms(pairs, ranks, near, far, paired):
    owned, width, _ = near.shape
    return pl.pallas_call(
        other_body,
        out_shape=(halves(owned, width, BF16), halves(owned, width, BF16)),
        in_specs=[in_place(), in_place(), in_vmem(), in_vmem(), in_vmem()],
        out_specs=(in_vmem(), in_vmem()),
        scratch_shapes=table_scratch(2 * owned, pairs, ranks),
        cost_estimate=cost(2 * owned),
        compiler_params=pltpu.CompilerParams(vmem_limit_bytes=8 * 2**20),
        name="other_terms",
    )(pairs, ranks, near, far, paired)


def passed_along(value, axis, steps):
    count = lax.axis_size(axis)
    return lax.ppermute(value, axis, [(source, (source + steps) % count) for source in range(count)])


def shards(panels, aux_counts, pair_list, pair_ranks, amplitudes):
    side = lax.axis_index("aux")
    pairs = kept_in_hbm(pair_list.T)
    ranks = kept_in_hbm(pair_ranks)
    far_amps = passed_along(amplitudes, "blk", -2)
    near_amps = passed_along(amplitudes, "blk", -1)
    paired, early = loaded(kept_in_hbm(aux_counts), pairs, ranks, kept_in_hbm(amplitudes), kept_in_hbm(panels))
    near, far = other_terms(pairs, ranks, near_amps, far_amps, paired)
    late = own_terms(pairs, ranks, amplitudes, paired, far)
    far = passed_along(far, "blk", 2)
    near = passed_along(near, "blk", 1)

    def half(value, which):
        return lax.dynamic_index_in_dim(value, which, 0, keepdims=False).astype(F32)

    def summed(which):
        own = jnp.concatenate([half(early, which), half(late, which)], axis=0)
        return own + half(near, which) + half(far, which)

    received = passed_along(summed(1 - side).astype(BF16), "aux", 1)
    return summed(side) + received.astype(F32)


def solution(mesh):
    placed = (P(None, ("blk", "aux"), None, None), P(), P(), P(), P("blk", None, None))
    return jax.shard_map(
        shards, mesh=mesh, in_specs=placed, out_specs=P("blk", "aux", None), check_vma=False
    )
```

time: 40.9 us -> 42.7 us (1.044)
  waiting for transfers between devices: 12 us -> 14.8 us
  Pallas kernels: 17.7 us -> 15.4 us
  starting transfers between devices: 10.2 us -> 11.4 us
    ppermute x5, waiting for transfers between devices: 12 us -> 14.8 us  [passed_along(): lax.ppermute(value, axis, [(source, (source + steps) % count) for source...]
    pallas_call x3, Pallas kernels: 17.7 us -> 15.4 us  [the longest x1 7.25 us: other_terms(): pl.pallas_call(other_body, out_shape=(halves(owned, width, BF16), halves(...]
    ppermute x5, starting transfers between devices: 10.2 us -> 11.4 us  [passed_along(): lax.ppermute(value, axis, [(source, (source + steps) % count) for source...]
  transfers between devices with their start and end apart: 5 -> 5, of which waited for: 4 -> 3; matrix products, arithmetic and copies ran while one was open for 0% -> 0% of each run, Pallas kernels for 20% -> 13%
where the time goes in v3:
time: 42.7 us; the launch traced here: 42.5 us
  Pallas kernels  15.4 us (36%)
  waiting for transfers between devices  14.8 us (35%)
  starting transfers between devices  11.4 us (27%)
  local copies, waits for them, and re-layouts  0.76 us (2%)
    ppermute x5, waiting for transfers between devices, passed_along(): lax.ppermute(value, axis, [(source, (source + steps) % count) for source...  14.8 us
    ppermute x5, starting transfers between devices, passed_along(): lax.ppermute(value, axis, [(source, (source + steps) % count) for source...  11.4 us
    pallas_call x1, Pallas kernels, other_terms(): pl.pallas_call(other_body, out_shape=(halves(owned, width, BF16), halves(...  7.25 us
    pallas_call x1, Pallas kernels, loaded(): pl.pallas_call(load_body, out_shape=(pltpu.VMEM((orbitals, slots // 2, 2,...  5.51 us
    pallas_call x1, Pallas kernels, own_terms(): pl.pallas_call(own_body, out_shape=halves(owned - EARLY, width, F32), in_...  2.61 us
  transfers between devices with their start and end apart: 5, of which 3 were waited for; matrix products, arithmetic and copies ran while one was open for 0% of the time, Pallas kernels for 13%

profile of v3, /device:TPU:4, one launch (start us, length us, event | category | flops | bytes accessed | tf_op | source)
XLA Modules:
  0.0 42.5 jit_solution(14745408468533725242)
XLA Ops:
  0.0 8.4 %collective-permute-start = (bf16[4,120,120]{2,1,0:T(8,128)(2,1)}, bf16[4,120,120]{2,1,0:T(8,128)(2,1)S(1)}, u32[]{:S(2)}, u32[]{:S(2)}) collective-permute-start(bf16[4,120,120]{2,1,0:T(8,128)(2,1)} %amps.3), channel_id=1, source_target_pairs={{0,254},{2,0},{4,2},{6,4},{8,6},{10,8},{12,10},{14,12},{16,14},{18... | collective-permute-start | bytes 345608 | tf_op jit(solution)/shard_map/ppermute | solution.py:211
  8.4 0.7 %collective-permute-start.1 = (bf16[4,120,120]{2,1,0:T(8,128)(2,1)}, bf16[4,120,120]{2,1,0:T(8,128)(2,1)S(1)}, u32[]{:S(2)}, u32[]{:S(2)}) collective-permute-start(bf16[4,120,120]{2,1,0:T(8,128)(2,1)} %amps.3), channel_id=1, source_target_pairs={{0,252},{2,254},{4,0},{6,2},{8,4},{10,6},{12,8},{14,10},{16,12},{1... | collective-permute-start | bytes 345608 | tf_op jit(solution)/shard_map/ppermute | solution.py:211
  9.1 5.5 %loaded.1 = (bf16[4,22,2,128,128]{4,3,2,1,0:T(8,128)(2,1)S(1)}, f32[2,2,60,120]{3,2,1,0:T(8,128)S(1)}) custom-call(s32[256]{0:T(256)} %counts.1, s32[2,512]{1,0:T(2,128)} %bitcast.21, s32[512]{0:T(512)} %ranks.5, bf16[4,120,120]{2,1,0:T(8,128)(2,1)} %amps.3, bf16[4,44,120,120]{3,2,1,0:T(8,128)(2,1)} %panels.1), custom_call_target="tpu_custom_call" | custom-call | flops 3000000000 | bytes 5000000 | tf_op jit(solution)/shard_map/loaded/pallas_call | solution.py:148
  14.7 0.0 collective-permute-done.near
  14.7 0.0 collective-permute-done.1.far
  14.7 0.0 copy-start
  14.7 7.2 %other_terms.1 = (bf16[2,4,60,120]{3,2,1,0:T(8,128)(2,1)S(1)}, bf16[2,4,60,120]{3,2,1,0:T(8,128)(2,1)S(1)}) custom-call(s32[2,512]{1,0:T(2,128)} %bitcast.22, s32[512]{0:T(512)} %ranks.5, bf16[4,120,120]{2,1,0:T(8,128)(2,1)S(1)} %collective-permute-done.near, bf16[4,120,120]{2,1,0:T(8,128)(2,1)S(1)} %collective-permute-done.1.far, ...), custom_call_target="tpu_custom_call" | custom-call | flops 8000000000 | bytes 5000000 | tf_op jit(solution)/shard_map/other_terms/pallas_call | solution.py:197
  22.0 0.0 copy-done
  22.0 2.6 %own_terms.1 = f32[2,2,60,120]{3,2,1,0:T(8,128)S(1)} custom-call(s32[2,512]{1,0:T(2,128)} %bitcast.23, s32[512]{0:T(512)} %ranks.5, bf16[4,120,120]{2,1,0:T(8,128)(2,1)S(1)} %copy-done, bf16[4,22,2,128,128]{4,3,2,1,0:T(8,128)(2,1)S(1)} %get-tuple-element.10.paired, bf16[2,4,60,120]{3,2,1,0:T(8,128)(2,1)S(1)} %get-tuple-element.11.after), custom_call_target="tpu_custom_call" | custom-call | flops 8000000000 | bytes 5000000 | tf_op jit(solution)/shard_map/own_terms/pallas_call | solution.py:183
  24.6 1.4 %collective-permute-start.3 = (bf16[2,4,60,120]{3,2,1,0:T(8,128)(2,1)S(1)}, bf16[2,4,60,120]{3,2,1,0:T(8,128)(2,1)S(1)}, u32[]{:S(2)}, u32[]{:S(2)}) collective-permute-start(bf16[2,4,60,120]{3,2,1,0:T(8,128)(2,1)S(1)} %get-tuple-element.11.after), channel_id=1, source_target_pairs={{0,4},{2,6},{4,8},{6,10},{8,12},{10,14},{12,16},{14,18},{16,20},{1... | collective-permute-start | bytes 345608 | tf_op jit(solution)/shard_map/ppermute | solution.py:211
  26.0 0.0 collective-permute-start.2
  26.0 9.4 %collective-permute-done.3 = bf16[2,4,60,120]{3,2,1,0:T(8,128)(2,1)S(1)} collective-permute-done((bf16[2,4,60,120]{3,2,1,0:T(8,128)(2,1)S(1)}, bf16[2,4,60,120]{3,2,1,0:T(8,128)(2,1)S(1)}, u32[]{:S(2)}, u32[]{:S(2)}) %collective-permute-start.3) | collective-permute-done | bytes 115232 | tf_op jit(solution)/shard_map/ppermute | solution.py:211
  35.4 0.5 %collective-permute-done.2 = bf16[2,4,60,120]{3,2,1,0:T(8,128)(2,1)S(1)} collective-permute-done((bf16[2,4,60,120]{3,2,1,0:T(8,128)(2,1)S(1)}, bf16[2,4,60,120]{3,2,1,0:T(8,128)(2,1)S(1)}, u32[]{:S(2)}, u32[]{:S(2)}) %collective-permute-start.2) | collective-permute-done | bytes 115232 | tf_op jit(solution)/shard_map/ppermute | solution.py:211
  35.9 0.9 %collective-permute-start.4 = (bf16[4,60,120]{2,1,0:T(8,128)(2,1)S(1)}, bf16[4,60,120]{2,1,0:T(8,128)(2,1)S(1)}, u32[]{:S(2)}, u32[]{:S(2)}) collective-permute-start(bf16[4,60,120]{2,1,0:T(8,128)(2,1)S(1)} %fusion.3), channel_id=1, source_target_pairs={{0,1},{1,0},{2,3},{3,2},{4,5},{5,4},{6,7},{7,6},{8,9},{9,8},{10,11... | collective-permute-start | bytes 172808 | tf_op jit(solution)/shard_map/ppermute | solution.py:211
  36.8 5.0 %collective-permute-done.4 = bf16[4,60,120]{2,1,0:T(8,128)(2,1)S(1)} collective-permute-done((bf16[4,60,120]{2,1,0:T(8,128)(2,1)S(1)}, bf16[4,60,120]{2,1,0:T(8,128)(2,1)S(1)}, u32[]{:S(2)}, u32[]{:S(2)}) %collective-permute-start.4) | collective-permute-done | bytes 57632 | tf_op jit(solution)/shard_map/ppermute | solution.py:211
  41.8 0.7 %copy.6 = f32[4,60,120]{2,0,1:T(4,128)} copy(f32[4,60,120]{2,1,0:T(8,128)S(1)} %fusion.1) | data formatting | bytes 230400 | tf_op jit(solution)/shard_map/add | solution.py:234
  (4 shorter events, 0.1 us)
Async XLA Ops:
  0.0 14.7 %collective-permute-start = (bf16[4,120,120]{2,1,0:T(8,128)(2,1)}, bf16[4,120,120]{2,1,0:T(8,128)(2,1)S(1)}, u32[]{:S(2)}, u32[]{:S(2)}) collective-permute-start(bf16[4,120,120]{2,1,0:T(8,128)(2,1)} %amps.3), channel_id=1, source_target_pairs={{0,254},{2,0},{4,2},{6,4},{8,6},{10,8},{12,10},{14,12},{16,14},{18... | collective-permute-start | bytes 345608 | tf_op jit(solution)/shard_map/ppermute | solution.py:211
  8.4 6.3 %collective-permute-start.1 = (bf16[4,120,120]{2,1,0:T(8,128)(2,1)}, bf16[4,120,120]{2,1,0:T(8,128)(2,1)S(1)}, u32[]{:S(2)}, u32[]{:S(2)}) collective-permute-start(bf16[4,120,120]{2,1,0:T(8,128)(2,1)} %amps.3), channel_id=1, source_target_pairs={{0,252},{2,254},{4,0},{6,2},{8,4},{10,6},{12,8},{14,10},{16,12},{1... | collective-permute-start | bytes 345608 | tf_op jit(solution)/shard_map/ppermute | solution.py:211
  14.7 7.3 %copy-start = (bf16[4,120,120]{2,1,0:T(8,128)(2,1)S(1)}, bf16[4,120,120]{2,1,0:T(8,128)(2,1)}, u32[]{:S(2)}) copy-start(bf16[4,120,120]{2,1,0:T(8,128)(2,1)} %amps.3) | copy-start | bytes 345604
  24.6 10.8 %collective-permute-start.3 = (bf16[2,4,60,120]{3,2,1,0:T(8,128)(2,1)S(1)}, bf16[2,4,60,120]{3,2,1,0:T(8,128)(2,1)S(1)}, u32[]{:S(2)}, u32[]{:S(2)}) collective-permute-start(bf16[2,4,60,120]{3,2,1,0:T(8,128)(2,1)S(1)} %get-tuple-element.11.after), channel_id=1, source_target_pairs={{0,4},{2,6},{4,8},{6,10},{8,12},{10,14},{12,16},{14,18},{16,20},{1... | collective-permute-start | bytes 345608 | tf_op jit(solution)/shard_map/ppermute | solution.py:211
  26.0 9.9 %collective-permute-start.2 = (bf16[2,4,60,120]{3,2,1,0:T(8,128)(2,1)S(1)}, bf16[2,4,60,120]{3,2,1,0:T(8,128)(2,1)S(1)}, u32[]{:S(2)}, u32[]{:S(2)}) collective-permute-start(bf16[2,4,60,120]{3,2,1,0:T(8,128)(2,1)S(1)} %get-tuple-element.12), channel_id=1, source_target_pairs={{0,2},{2,4},{4,6},{6,8},{8,10},{10,12},{12,14},{14,16},{16,18},{18... | collective-permute-start | bytes 345608 | tf_op jit(solution)/shard_map/ppermute | solution.py:211
  35.9 5.9 %collective-permute-start.4 = (bf16[4,60,120]{2,1,0:T(8,128)(2,1)S(1)}, bf16[4,60,120]{2,1,0:T(8,128)(2,1)S(1)}, u32[]{:S(2)}, u32[]{:S(2)}) collective-permute-start(bf16[4,60,120]{2,1,0:T(8,128)(2,1)S(1)} %fusion.3), channel_id=1, source_target_pairs={{0,1},{1,0},{2,3},{3,2},{4,5},{5,4},{6,7},{7,6},{8,9},{9,8},{10,11... | collective-permute-start | bytes 172808 | tf_op jit(solution)/shard_map/ppermute | solution.py:211

commit v4 on v3

--- a/solution.py
+++ b/solution.py
@@ -1,3 +1,4 @@
+import functools
 import jax
 import jax.numpy as jnp
 from jax import lax
@@ -94,7 +95,7 @@
     terms(work, paired, squares, pairs_s, ranks_s)
 
 
-def own_body(pairs, ranks, amps, paired, after, out, squares, pairs_s, ranks_s, sems):
+def group_body(first, hops, pairs, ranks, amps, paired, after, out, squares, pairs_s, ranks_s, sems):
     del after
     owned = amps.shape[0]
     small = table_copies(pairs, ranks, pairs_s, ranks_s, sems)
@@ -102,24 +103,8 @@
         copy.start()
     for copy in small:
         copy.wait()
-    block = lax.axis_index("blk")
-    work = [(block * owned + p, amps[p], stored(out, p - EARLY)) for p in range(EARLY, owned)]
-    terms(work, paired, squares, pairs_s, ranks_s)
-
-
-def other_body(pairs, ranks, near, far, paired, near_out, far_out, squares, pairs_s, ranks_s, sems):
-    owned = near.shape[0]
-    blocks = lax.axis_size("blk")
-    block = lax.axis_index("blk")
-    small = table_copies(pairs, ranks, pairs_s, ranks_s, sems)
-    for copy in small:
-        copy.start()
-    for copy in small:
-        copy.wait()
-    work = []
-    for amps, out, hops in ((far, far_out, 2), (near, near_out, 1)):
-        start = (block + hops) % blocks * owned
-        work += [(start + p, amps[p], stored(out, p)) for p in range(owned)]
+    start = (lax.axis_index("blk") + hops) % lax.axis_size("blk") * owned
+    work = [(start + p, amps[p], stored(out, p - first)) for p in range(first, owned)]
     terms(work, paired, squares, pairs_s, ranks_s)
 
 
@@ -178,32 +163,18 @@
     ]
 
 
-def own_terms(pairs, ranks, amps, paired, after):
+def group_terms(first, hops, kind, pairs, ranks, amps, paired, after):
     owned, width, _ = amps.shape
+    anywhere = pl.BlockSpec(memory_space=pl.ANY)
     return pl.pallas_call(
-        own_body,
-        out_shape=halves(owned - EARLY, width, F32),
-        in_specs=[in_place(), in_place(), in_vmem(), in_vmem(), pl.BlockSpec(memory_space=pl.ANY)],
+        functools.partial(group_body, first, hops),
+        out_shape=halves(owned - first, width, kind),
+        in_specs=[anywhere, anywhere, in_vmem(), in_vmem(), anywhere],
         out_specs=in_vmem(),
-        scratch_shapes=table_scratch(owned - EARLY, pairs, ranks),
-        cost_estimate=cost(2 * owned),
+        scratch_shapes=table_scratch(owned - first, pairs, ranks),
+        cost_estimate=cost(owned - first),
         compiler_params=pltpu.CompilerParams(vmem_limit_bytes=8 * 2**20),
-        name="own_terms",
     )(pairs, ranks, amps, paired, after)
-
-
-def other_terms(pairs, ranks, near, far, paired):
-    owned, width, _ = near.shape
-    return pl.pallas_call(
-        other_body,
-        out_shape=(halves(owned, width, BF16), halves(owned, width, BF16)),
-        in_specs=[in_place(), in_place(), in_vmem(), in_vmem(), in_vmem()],
-        out_specs=(in_vmem(), in_vmem()),
-        scratch_shapes=table_scratch(2 * owned, pairs, ranks),
-        cost_estimate=cost(2 * owned),
-        compiler_params=pltpu.CompilerParams(vmem_limit_bytes=8 * 2**20),
-        name="other_terms",
-    )(pairs, ranks, near, far, paired)
 
 
 def passed_along(value, axis, steps):
@@ -213,13 +184,16 @@
 
 def shards(panels, aux_counts, pair_list, pair_ranks, amplitudes):
     side = lax.axis_index("aux")
-    pairs = kept_in_hbm(pair_list.T)
-    ranks = kept_in_hbm(pair_ranks)
+    pairs = pair_list.T
+    ranks = pair_ranks
     far_amps = passed_along(amplitudes, "blk", -2)
     near_amps = passed_along(amplitudes, "blk", -1)
-    paired, early = loaded(kept_in_hbm(aux_counts), pairs, ranks, kept_in_hbm(amplitudes), kept_in_hbm(panels))
-    near, far = other_terms(pairs, ranks, near_amps, far_amps, paired)
-    late = own_terms(pairs, ranks, amplitudes, paired, far)
+    paired, early = loaded(
+        kept_in_hbm(aux_counts), kept_in_hbm(pairs), kept_in_hbm(ranks), kept_in_hbm(amplitudes), kept_in_hbm(panels)
+    )
+    far = group_terms(0, 2, BF16, pairs, ranks, far_amps, paired, early)
+    near = group_terms(0, 1, BF16, pairs, ranks, near_amps, paired, far)
+    late = group_terms(EARLY, 0, F32, pairs, ranks, amplitudes, paired, near)
     far = passed_along(far, "blk", 2)
     near = passed_along(near, "blk", 1)
 

time: 42.7 us -> 43.3 us (1.014)
  the two profiles are of different devices: /device:TPU:4 before, /device:TPU:1 now
where the time goes in v4:
time: 43.3 us
  Pallas kernels  16 us (37%)
  starting transfers between devices  14 us (32%)
  waiting for transfers between devices  12.3 us (28%)
  local copies, waits for them, and re-layouts  0.77 us (2%)
    ppermute x5, starting transfers between devices, passed_along(): lax.ppermute(value, axis, [(source, (source + steps) % count) for source...  14 us
    ppermute x5, waiting for transfers between devices, passed_along(): lax.ppermute(value, axis, [(source, (source + steps) % count) for source...  12.3 us
    pallas_call x3, Pallas kernels, group_terms(): pl.pallas_call(functools.partial(group_body, first, hops), out_shape=halv...  10.5 us
    pallas_call x1, Pallas kernels, loaded(): pl.pallas_call(load_body, out_shape=(pltpu.VMEM((orbitals, slots // 2, 2,...  5.51 us
  transfers between devices with their start and end apart: 5, of which 3 were waited for; matrix products, arithmetic and copies ran while one was open for 0% of the time, Pallas kernels for 22%

profile of v4, /device:TPU:1, one launch (start us, length us, event | category | flops | bytes accessed | tf_op | source)
XLA Modules:
  0.0 43.3 jit_solution(13591021261204298188)
XLA Ops:
  0.0 0.0 copy-start.1
  0.0 0.0 copy-start.2
  0.0 9.8 %collective-permute-start.1 = (bf16[4,120,120]{2,1,0:T(8,128)(2,1)}, bf16[4,120,120]{2,1,0:T(8,128)(2,1)S(1)}, u32[]{:S(2)}, u32[]{:S(2)}) collective-permute-start(bf16[4,120,120]{2,1,0:T(8,128)(2,1)} %amps.3), channel_id=1, source_target_pairs={{0,252},{2,254},{4,0},{6,2},{8,4},{10,6},{12,8},{14,10},{16,12},{1... | collective-permute-start | bytes 345608 | tf_op jit(solution)/shard_map/ppermute | solution.py:182
  9.8 1.0 %collective-permute-start = (bf16[4,120,120]{2,1,0:T(8,128)(2,1)}, bf16[4,120,120]{2,1,0:T(8,128)(2,1)S(1)}, u32[]{:S(2)}, u32[]{:S(2)}) collective-permute-start(bf16[4,120,120]{2,1,0:T(8,128)(2,1)} %amps.3), channel_id=1, source_target_pairs={{0,254},{2,0},{4,2},{6,4},{8,6},{10,8},{12,10},{14,12},{16,14},{18... | collective-permute-start | bytes 345608 | tf_op jit(solution)/shard_map/ppermute | solution.py:182
  10.7 5.5 %loaded.1 = (bf16[4,22,2,128,128]{4,3,2,1,0:T(8,128)(2,1)S(1)}, f32[2,2,60,120]{3,2,1,0:T(8,128)S(1)}) custom-call(s32[256]{0:T(256)} %counts.1, s32[2,512]{1,0:T(2,128)} %bitcast.21, s32[512]{0:T(512)} %ranks.7, bf16[4,120,120]{2,1,0:T(8,128)(2,1)} %amps.3, bf16[4,44,120,120]{3,2,1,0:T(8,128)(2,1)} %panels.1), custom_call_target="tpu_custom_call" | custom-call | flops 3000000000 | bytes 5000000 | tf_op jit(solution)/shard_map/loaded/pallas_call | solution.py:133
  16.3 0.0 collective-permute-done.1.amps
  16.3 0.0 copy-done.1
  16.3 0.0 copy-done.2
  16.3 4.0 %shard_map.55.after = bf16[2,4,60,120]{3,2,1,0:T(8,128)(2,1)S(1)} custom-call(s32[2,512]{1,0:T(2,128)S(1)} %bitcast.22, s32[512]{0:T(512)S(1)} %copy-done.2, bf16[4,120,120]{2,1,0:T(8,128)(2,1)S(1)} %collective-permute-done.1.amps, bf16[4,22,2,128,128]{4,3,2,1,0:T(8,128)(2,1)S(1)} %get-tuple-element.8.paired, f32[2,2,60,120]{3,2,1,0:T(8,128)S(1)} %get-tuple-element.7.after), custom_call_target="tpu_custom_call" | custom-call | flops 4000000000 | bytes 5000000 | tf_op jit(solution)/shard_map/pallas_call | solution.py:169
  20.3 0.0 copy-start
  20.3 0.0 collective-permute-done.amps
  20.3 4.0 %shard_map.56.after = bf16[2,4,60,120]{3,2,1,0:T(8,128)(2,1)S(1)} custom-call(s32[2,512]{1,0:T(2,128)S(1)} %bitcast.23, s32[512]{0:T(512)S(1)} %copy-done.2, bf16[4,120,120]{2,1,0:T(8,128)(2,1)S(1)} %collective-permute-done.amps, bf16[4,22,2,128,128]{4,3,2,1,0:T(8,128)(2,1)S(1)} %get-tuple-element.8.paired, bf16[2,4,60,120]{3,2,1,0:T(8,128)(2,1)S(1)} %shard_map.55.after), custom_call_target="tpu_custom_call" | custom-call | flops 4000000000 | bytes 5000000 | tf_op jit(solution)/shard_map/pallas_call | solution.py:169
  24.3 0.0 copy-done
  24.3 2.5 %shard_map.57 = f32[2,2,60,120]{3,2,1,0:T(8,128)S(1)} custom-call(s32[2,512]{1,0:T(2,128)S(1)} %bitcast.24, s32[512]{0:T(512)S(1)} %copy-done.2, bf16[4,120,120]{2,1,0:T(8,128)(2,1)S(1)} %copy-done, bf16[4,22,2,128,128]{4,3,2,1,0:T(8,128)(2,1)S(1)} %get-tuple-element.8.paired, bf16[2,4,60,120]{3,2,1,0:T(8,128)(2,1)S(1)} %shard_map.56.after), custom_call_target="tpu_custom_call" | custom-call | flops 2000000000 | bytes 5000000 | tf_op jit(solution)/shard_map/pallas_call | solution.py:169
  26.8 0.9 %collective-permute-start.2 = (bf16[2,4,60,120]{3,2,1,0:T(8,128)(2,1)S(1)}, bf16[2,4,60,120]{3,2,1,0:T(8,128)(2,1)S(1)}, u32[]{:S(2)}, u32[]{:S(2)}) collective-permute-start(bf16[2,4,60,120]{3,2,1,0:T(8,128)(2,1)S(1)} %shard_map.56.after), channel_id=1, source_target_pairs={{0,2},{2,4},{4,6},{6,8},{8,10},{10,12},{12,14},{14,16},{16,18},{18... | collective-permute-start | bytes 345608 | tf_op jit(solution)/shard_map/ppermute | solution.py:182
  27.7 0.0 collective-permute-start.3
  27.7 2.6 %collective-permute-done.2 = bf16[2,4,60,120]{3,2,1,0:T(8,128)(2,1)S(1)} collective-permute-done((bf16[2,4,60,120]{3,2,1,0:T(8,128)(2,1)S(1)}, bf16[2,4,60,120]{3,2,1,0:T(8,128)(2,1)S(1)}, u32[]{:S(2)}, u32[]{:S(2)}) %collective-permute-start.2) | collective-permute-done | bytes 115232 | tf_op jit(solution)/shard_map/ppermute | solution.py:182
  30.4 7.4 %collective-permute-done.3 = bf16[2,4,60,120]{3,2,1,0:T(8,128)(2,1)S(1)} collective-permute-done((bf16[2,4,60,120]{3,2,1,0:T(8,128)(2,1)S(1)}, bf16[2,4,60,120]{3,2,1,0:T(8,128)(2,1)S(1)}, u32[]{:S(2)}, u32[]{:S(2)}) %collective-permute-start.3) | collective-permute-done | bytes 115232 | tf_op jit(solution)/shard_map/ppermute | solution.py:182
  37.8 2.4 %collective-permute-start.4 = (bf16[4,60,120]{2,1,0:T(8,128)(2,1)S(1)}, bf16[4,60,120]{2,1,0:T(8,128)(2,1)S(1)}, u32[]{:S(2)}, u32[]{:S(2)}) collective-permute-start(bf16[4,60,120]{2,1,0:T(8,128)(2,1)S(1)} %fusion.3), channel_id=1, source_target_pairs={{0,1},{1,0},{2,3},{3,2},{4,5},{5,4},{6,7},{7,6},{8,9},{9,8},{10,11... | collective-permute-start | bytes 172808 | tf_op jit(solution)/shard_map/ppermute | solution.py:182
  40.2 2.3 %collective-permute-done.4 = bf16[4,60,120]{2,1,0:T(8,128)(2,1)S(1)} collective-permute-done((bf16[4,60,120]{2,1,0:T(8,128)(2,1)S(1)}, bf16[4,60,120]{2,1,0:T(8,128)(2,1)S(1)}, u32[]{:S(2)}, u32[]{:S(2)}) %collective-permute-start.4) | collective-permute-done | bytes 57632 | tf_op jit(solution)/shard_map/ppermute | solution.py:182
  42.5 0.7 %copy.6 = f32[4,60,120]{2,0,1:T(4,128)} copy(f32[4,60,120]{2,1,0:T(8,128)S(1)} %fusion.1) | data formatting | bytes 230400 | tf_op jit(solution)/shard_map/add | solution.py:208
  (4 shorter events, 0.1 us)
Async XLA Ops:
  0.0 16.3 %copy-start.1 = (s32[512,2]{0,1:T(2,128)S(1)}, s32[512,2]{0,1:T(2,128)}, u32[]{:S(2)}) copy-start(s32[512,2]{0,1:T(2,128)} %param.7) | copy-start | bytes 12292
  0.0 16.3 %copy-start.2 = (s32[512]{0:T(512)S(1)}, s32[512]{0:T(512)}, u32[]{:S(2)}) copy-start(s32[512]{0:T(512)} %ranks.7) | copy-start | bytes 6148
  0.0 16.3 %collective-permute-start.1 = (bf16[4,120,120]{2,1,0:T(8,128)(2,1)}, bf16[4,120,120]{2,1,0:T(8,128)(2,1)S(1)}, u32[]{:S(2)}, u32[]{:S(2)}) collective-permute-start(bf16[4,120,120]{2,1,0:T(8,128)(2,1)} %amps.3), channel_id=1, source_target_pairs={{0,252},{2,254},{4,0},{6,2},{8,4},{10,6},{12,8},{14,10},{16,12},{1... | collective-permute-start | bytes 345608 | tf_op jit(solution)/shard_map/ppermute | solution.py:182
  9.8 10.5 %collective-permute-start = (bf16[4,120,120]{2,1,0:T(8,128)(2,1)}, bf16[4,120,120]{2,1,0:T(8,128)(2,1)S(1)}, u32[]{:S(2)}, u32[]{:S(2)}) collective-permute-start(bf16[4,120,120]{2,1,0:T(8,128)(2,1)} %amps.3), channel_id=1, source_target_pairs={{0,254},{2,0},{4,2},{6,4},{8,6},{10,8},{12,10},{14,12},{16,14},{18... | collective-permute-start | bytes 345608 | tf_op jit(solution)/shard_map/ppermute | solution.py:182
  20.3 4.0 %copy-start = (bf16[4,120,120]{2,1,0:T(8,128)(2,1)S(1)}, bf16[4,120,120]{2,1,0:T(8,128)(2,1)}, u32[]{:S(2)}) copy-start(bf16[4,120,120]{2,1,0:T(8,128)(2,1)} %amps.3) | copy-start | bytes 345604
  26.8 3.5 %collective-permute-start.2 = (bf16[2,4,60,120]{3,2,1,0:T(8,128)(2,1)S(1)}, bf16[2,4,60,120]{3,2,1,0:T(8,128)(2,1)S(1)}, u32[]{:S(2)}, u32[]{:S(2)}) collective-permute-start(bf16[2,4,60,120]{3,2,1,0:T(8,128)(2,1)S(1)} %shard_map.56.after), channel_id=1, source_target_pairs={{0,2},{2,4},{4,6},{6,8},{8,10},{10,12},{12,14},{14,16},{16,18},{18... | collective-permute-start | bytes 345608 | tf_op jit(solution)/shard_map/ppermute | solution.py:182
  27.7 10.0 %collective-permute-start.3 = (bf16[2,4,60,120]{3,2,1,0:T(8,128)(2,1)S(1)}, bf16[2,4,60,120]{3,2,1,0:T(8,128)(2,1)S(1)}, u32[]{:S(2)}, u32[]{:S(2)}) collective-permute-start(bf16[2,4,60,120]{3,2,1,0:T(8,128)(2,1)S(1)} %shard_map.55.after), channel_id=1, source_target_pairs={{0,4},{2,6},{4,8},{6,10},{8,12},{10,14},{12,16},{14,18},{16,20},{1... | collective-permute-start | bytes 345608 | tf_op jit(solution)/shard_map/ppermute | solution.py:182
  37.8 4.7 %collective-permute-start.4 = (bf16[4,60,120]{2,1,0:T(8,128)(2,1)S(1)}, bf16[4,60,120]{2,1,0:T(8,128)(2,1)S(1)}, u32[]{:S(2)}, u32[]{:S(2)}) collective-permute-start(bf16[4,60,120]{2,1,0:T(8,128)(2,1)S(1)} %fusion.3), channel_id=1, source_target_pairs={{0,1},{1,0},{2,3},{3,2},{4,5},{5,4},{6,7},{7,6},{8,9},{9,8},{10,11... | collective-permute-start | bytes 172808 | tf_op jit(solution)/shard_map/ppermute | solution.py:182

commit v5 on v4

--- a/solution.py
+++ b/solution.py
@@ -9,7 +9,7 @@
 F32, BF16 = jnp.float32, jnp.bfloat16
 SLAB = 128
 STEP = 2
-EARLY = 2
+EARLY = 1
 
 
 def table_copies(pairs, ranks, pairs_s, ranks_s, sems):
@@ -57,10 +57,12 @@
 
 
 def stored(out, p):
+    lower = lax.axis_index("aux")
+
     def put(value):
         cut = value.shape[0] // 2
-        out[0, p] = value[:cut].astype(out.dtype)
-        out[1, p] = value[cut:].astype(out.dtype)
+        out[lower, p] = value[:cut].astype(out.dtype)
+        out[1 - lower, p] = value[cut:].astype(out.dtype)
 
     return put
 
@@ -182,8 +184,15 @@
     return lax.ppermute(value, axis, [(source, (source + steps) % count) for source in range(count)])
 
 
+def passed_across(value, steps):
+    blocks = lax.axis_size("blk")
+    route = [
+        (2 * block + side, 2 * ((block + steps) % blocks) + 1 - side) for block in range(blocks) for side in range(2)
+    ]
+    return lax.ppermute(value, ("blk", "aux"), route)
+
+
 def shards(panels, aux_counts, pair_list, pair_ranks, amplitudes):
-    side = lax.axis_index("aux")
     pairs = pair_list.T
     ranks = pair_ranks
     far_amps = passed_along(amplitudes, "blk", -2)
@@ -194,18 +203,16 @@
     far = group_terms(0, 2, BF16, pairs, ranks, far_amps, paired, early)
     near = group_terms(0, 1, BF16, pairs, ranks, near_amps, paired, far)
     late = group_terms(EARLY, 0, F32, pairs, ranks, amplitudes, paired, near)
-    far = passed_along(far, "blk", 2)
-    near = passed_along(near, "blk", 1)
-
-    def half(value, which):
-        return lax.dynamic_index_in_dim(value, which, 0, keepdims=False).astype(F32)
-
-    def summed(which):
-        own = jnp.concatenate([half(early, which), half(late, which)], axis=0)
-        return own + half(near, which) + half(far, which)
-
-    received = passed_along(summed(1 - side).astype(BF16), "aux", 1)
-    return summed(side) + received.astype(F32)
+    far_same = passed_along(far[0], "blk", 2)
+    far_other = passed_across(far[1], 2)
+    near_same = passed_along(near[0], "blk", 1)
+    near_other = passed_across(near[1], 1)
+    own = jnp.concatenate([early[0], late[0]], axis=0)
+    own_other = passed_across(jnp.concatenate([early[1], late[1]], axis=0).astype(BF16), 0)
+    total = own
+    for part in (far_same, far_other, near_same, near_other, own_other):
+        total = total + part.astype(F32)
+    return total
 
 
 def solution(mesh):

time: 43.3 us -> 39.8 us (0.919)
  waiting for transfers between devices: 12.3 us -> 6.81 us
  starting transfers between devices: 14 us -> 15.8 us
    ppermute x5 -> x4, waiting for transfers between devices: 12.3 us -> 4.73 us  [passed_along(): lax.ppermute(value, axis, [(source, (source + steps) % count) for source...]
    ppermute x0 -> x3, starting transfers between devices: none -> 3.68 us  [passed_across(): return lax.ppermute(value, ('blk', 'aux'), route)]
    ppermute x0 -> x3, waiting for transfers between devices: none -> 2.07 us  [passed_across(): return lax.ppermute(value, ('blk', 'aux'), route)]
    ppermute x5 -> x4, starting transfers between devices: 14 us -> 12.1 us  [passed_along(): lax.ppermute(value, axis, [(source, (source + steps) % count) for source...]
    pallas_call x1, Pallas kernels: 5.51 us -> 4.69 us  [loaded(): pl.pallas_call(load_body, out_shape=(pltpu.VMEM((orbitals, slots // 2, 2,...]
    pallas_call x3, Pallas kernels: 10.5 us -> 11.2 us  [group_terms(): pl.pallas_call(functools.partial(group_body, first, hops), out_shape=halv...]
  transfers between devices with their start and end apart: 5 -> 7, of which waited for: 3 -> 2; matrix products, arithmetic and copies ran while one was open for 0% -> 0% of each run, Pallas kernels for 22% -> 22%
where the time goes in v5:
time: 39.8 us; the launch traced here: 39.5 us
  Pallas kernels  15.9 us (40%)
  starting transfers between devices  15.8 us (40%)
  waiting for transfers between devices  6.81 us (17%)
  local copies, waits for them, and re-layouts  0.79 us (2%)
    ppermute x4, starting transfers between devices, passed_along(): lax.ppermute(value, axis, [(source, (source + steps) % count) for source...  12.1 us
    pallas_call x3, Pallas kernels, group_terms(): pl.pallas_call(functools.partial(group_body, first, hops), out_shape=halv...  11.2 us
    ppermute x4, waiting for transfers between devices, passed_along(): lax.ppermute(value, axis, [(source, (source + steps) % count) for source...  4.73 us
    pallas_call x1, Pallas kernels, loaded(): pl.pallas_call(load_body, out_shape=(pltpu.VMEM((orbitals, slots // 2, 2,...  4.69 us
    ppermute x3, starting transfers between devices, passed_across(): return lax.ppermute(value, ('blk', 'aux'), route)  3.68 us
    ppermute x3, waiting for transfers between devices, passed_across(): return lax.ppermute(value, ('blk', 'aux'), route)  2.07 us
  transfers between devices with their start and end apart: 7, of which 2 were waited for; matrix products, arithmetic and copies ran while one was open for 0% of the time, Pallas kernels for 22%

profile of v5, /device:TPU:1, one launch (start us, length us, event | category | flops | bytes accessed | tf_op | source)
XLA Modules:
  0.0 39.5 jit_solution(2154331794894799612)
XLA Ops:
  0.0 0.0 copy-start.2
  0.0 0.0 copy-start.1
  0.0 3.2 %collective-permute-start = (bf16[4,120,120]{2,1,0:T(8,128)(2,1)}, bf16[4,120,120]{2,1,0:T(8,128)(2,1)S(1)}, u32[]{:S(2)}, u32[]{:S(2)}) collective-permute-start(bf16[4,120,120]{2,1,0:T(8,128)(2,1)} %amps.3), channel_id=1, source_target_pairs={{0,254},{2,0},{4,2},{6,4},{8,6},{10,8},{12,10},{14,12},{16,14},{18... | collective-permute-start | bytes 345608 | tf_op jit(solution)/shard_map/ppermute | solution.py:184
  3.2 7.2 %collective-permute-start.1 = (bf16[4,120,120]{2,1,0:T(8,128)(2,1)}, bf16[4,120,120]{2,1,0:T(8,128)(2,1)S(1)}, u32[]{:S(2)}, u32[]{:S(2)}) collective-permute-start(bf16[4,120,120]{2,1,0:T(8,128)(2,1)} %amps.3), channel_id=1, source_target_pairs={{0,252},{2,254},{4,0},{6,2},{8,4},{10,6},{12,8},{14,10},{16,12},{1... | collective-permute-start | bytes 345608 | tf_op jit(solution)/shard_map/ppermute | solution.py:184
  10.5 4.7 %loaded.1 = (bf16[4,22,2,128,128]{4,3,2,1,0:T(8,128)(2,1)S(1)}, f32[2,1,60,120]{3,2,1,0:T(8,128)S(1)}) custom-call(s32[256]{0:T(256)} %counts.1, s32[2,512]{1,0:T(2,128)} %bitcast.17, s32[512]{0:T(512)} %ranks.7, bf16[4,120,120]{2,1,0:T(8,128)(2,1)} %amps.3, bf16[4,44,120,120]{3,2,1,0:T(8,128)(2,1)} %panels.1), custom_call_target="tpu_custom_call" | custom-call | flops 3000000000 | bytes 5000000 | tf_op jit(solution)/shard_map/loaded/pallas_call | solution.py:135
  15.2 0.0 collective-permute-done.1.amps
  15.2 0.0 copy-done.2
  15.2 0.0 copy-done.1
  15.2 4.0 %shard_map.55.after = bf16[2,4,60,120]{3,2,1,0:T(8,128)(2,1)S(1)} custom-call(s32[2,512]{1,0:T(2,128)S(1)} %bitcast.18, s32[512]{0:T(512)S(1)} %copy-done.2, bf16[4,120,120]{2,1,0:T(8,128)(2,1)S(1)} %collective-permute-done.1.amps, bf16[4,22,2,128,128]{4,3,2,1,0:T(8,128)(2,1)S(1)} %get-tuple-element.8.paired, f32[2,1,60,120]{3,2,1,0:T(8,128)S(1)} %get-tuple-element.7.after), custom_call_target="tpu_custom_call" | custom-call | flops 4000000000 | bytes 5000000 | tf_op jit(solution)/shard_map/pallas_call | solution.py:171
  19.2 0.0 copy-start
  19.2 0.0 collective-permute-done.amps
  19.2 4.0 %shard_map.56.after = bf16[2,4,60,120]{3,2,1,0:T(8,128)(2,1)S(1)} custom-call(s32[2,512]{1,0:T(2,128)S(1)} %bitcast.19, s32[512]{0:T(512)S(1)} %copy-done.2, bf16[4,120,120]{2,1,0:T(8,128)(2,1)S(1)} %collective-permute-done.amps, bf16[4,22,2,128,128]{4,3,2,1,0:T(8,128)(2,1)S(1)} %get-tuple-element.8.paired, bf16[2,4,60,120]{3,2,1,0:T(8,128)(2,1)S(1)} %shard_map.55.after), custom_call_target="tpu_custom_call" | custom-call | flops 4000000000 | bytes 5000000 | tf_op jit(solution)/shard_map/pallas_call | solution.py:171
  23.2 0.0 copy-done
  23.2 3.2 %shard_map.57 = f32[2,3,60,120]{3,2,1,0:T(8,128)S(1)} custom-call(s32[2,512]{1,0:T(2,128)S(1)} %bitcast.20, s32[512]{0:T(512)S(1)} %copy-done.2, bf16[4,120,120]{2,1,0:T(8,128)(2,1)S(1)} %copy-done, bf16[4,22,2,128,128]{4,3,2,1,0:T(8,128)(2,1)S(1)} %get-tuple-element.8.paired, bf16[2,4,60,120]{3,2,1,0:T(8,128)(2,1)S(1)} %shard_map.56.after), custom_call_target="tpu_custom_call" | custom-call | flops 3000000000 | bytes 5000000 | tf_op jit(solution)/shard_map/pallas_call | solution.py:171
  26.6 2.7 %collective-permute-start.6 = (bf16[4,60,120]{2,1,0:T(8,128)(2,1)S(1)}, bf16[4,60,120]{2,1,0:T(8,128)(2,1)S(1)}, u32[]{:S(2)}, u32[]{:S(2)}) collective-permute-start(bf16[4,60,120]{2,1,0:T(8,128)(2,1)S(1)} %pad_maximum_fusion), channel_id=1, source_target_pairs={{0,1},{1,0},{2,3},{3,2},{4,5},{5,4},{6,7},{7,6},{8,9},{9,8},{10,11... | collective-permute-start | bytes 172808 | tf_op jit(solution)/shard_map/ppermute | solution.py:192
  29.3 0.0 collective-permute-start.2
  29.3 0.0 collective-permute-start.3
  29.3 1.6 %collective-permute-start.4 = (bf16[4,60,120]{2,1,0:T(8,128)(2,1)S(1)}, bf16[4,60,120]{2,1,0:T(8,128)(2,1)S(1)}, u32[]{:S(2)}, u32[]{:S(2)}) collective-permute-start(bf16[4,60,120]{2,1,0:T(8,128)(2,1)S(1)} %get-tuple-element.11), channel_id=1, source_target_pairs={{0,2},{2,4},{4,6},{6,8},{8,10},{10,12},{12,14},{14,16},{16,18},{18... | collective-permute-start | bytes 172808 | tf_op jit(solution)/shard_map/ppermute | solution.py:184
  30.9 1.0 %collective-permute-start.5 = (bf16[4,60,120]{2,1,0:T(8,128)(2,1)S(1)}, bf16[4,60,120]{2,1,0:T(8,128)(2,1)S(1)}, u32[]{:S(2)}, u32[]{:S(2)}) collective-permute-start(bf16[4,60,120]{2,1,0:T(8,128)(2,1)S(1)} %get-tuple-element.12), channel_id=1, source_target_pairs={{0,3},{1,2},{2,5},{3,4},{4,7},{5,6},{6,9},{7,8},{8,11},{9,10},{10,... | collective-permute-start | bytes 172808 | tf_op jit(solution)/shard_map/ppermute | solution.py:192
  31.9 0.0 collective-permute-done.6
  31.9 4.7 %collective-permute-done.2 = bf16[4,60,120]{2,1,0:T(8,128)(2,1)S(1)} collective-permute-done((bf16[4,60,120]{2,1,0:T(8,128)(2,1)S(1)}, bf16[4,60,120]{2,1,0:T(8,128)(2,1)S(1)}, u32[]{:S(2)}, u32[]{:S(2)}) %collective-permute-start.2) | collective-permute-done | bytes 57632 | tf_op jit(solution)/shard_map/ppermute | solution.py:184
  36.6 2.1 %collective-permute-done.3 = bf16[4,60,120]{2,1,0:T(8,128)(2,1)S(1)} collective-permute-done((bf16[4,60,120]{2,1,0:T(8,128)(2,1)S(1)}, bf16[4,60,120]{2,1,0:T(8,128)(2,1)S(1)}, u32[]{:S(2)}, u32[]{:S(2)}) %collective-permute-start.3) | collective-permute-done | bytes 57632 | tf_op jit(solution)/shard_map/ppermute | solution.py:192
  38.7 0.0 collective-permute-done.4
  38.7 0.0 collective-permute-done.5
  38.7 0.1 fusion.3
  38.7 0.7 %copy.6 = f32[4,60,120]{2,0,1:T(4,128)} copy(f32[4,60,120]{2,1,0:T(8,128)S(1)} %fusion.3) | data formatting | bytes 230400 | tf_op jit(solution)/shard_map/add | solution.py:214
  (7 shorter events, 0.1 us)
Async XLA Ops:
  0.0 15.2 %copy-start.2 = (s32[512]{0:T(512)S(1)}, s32[512]{0:T(512)}, u32[]{:S(2)}) copy-start(s32[512]{0:T(512)} %ranks.7) | copy-start | bytes 6148
  0.0 15.2 %copy-start.1 = (s32[512,2]{0,1:T(2,128)S(1)}, s32[512,2]{0,1:T(2,128)}, u32[]{:S(2)}) copy-start(s32[512,2]{0,1:T(2,128)} %param.7) | copy-start | bytes 12292
  0.0 19.2 %collective-permute-start = (bf16[4,120,120]{2,1,0:T(8,128)(2,1)}, bf16[4,120,120]{2,1,0:T(8,128)(2,1)S(1)}, u32[]{:S(2)}, u32[]{:S(2)}) collective-permute-start(bf16[4,120,120]{2,1,0:T(8,128)(2,1)} %amps.3), channel_id=1, source_target_pairs={{0,254},{2,0},{4,2},{6,4},{8,6},{10,8},{12,10},{14,12},{16,14},{18... | collective-permute-start | bytes 345608 | tf_op jit(solution)/shard_map/ppermute | solution.py:184
  3.2 12.0 %collective-permute-start.1 = (bf16[4,120,120]{2,1,0:T(8,128)(2,1)}, bf16[4,120,120]{2,1,0:T(8,128)(2,1)S(1)}, u32[]{:S(2)}, u32[]{:S(2)}) collective-permute-start(bf16[4,120,120]{2,1,0:T(8,128)(2,1)} %amps.3), channel_id=1, source_target_pairs={{0,252},{2,254},{4,0},{6,2},{8,4},{10,6},{12,8},{14,10},{16,12},{1... | collective-permute-start | bytes 345608 | tf_op jit(solution)/shard_map/ppermute | solution.py:184
  19.2 4.0 %copy-start = (bf16[4,120,120]{2,1,0:T(8,128)(2,1)S(1)}, bf16[4,120,120]{2,1,0:T(8,128)(2,1)}, u32[]{:S(2)}) copy-start(bf16[4,120,120]{2,1,0:T(8,128)(2,1)} %amps.3) | copy-start | bytes 345604
  26.6 5.3 %collective-permute-start.6 = (bf16[4,60,120]{2,1,0:T(8,128)(2,1)S(1)}, bf16[4,60,120]{2,1,0:T(8,128)(2,1)S(1)}, u32[]{:S(2)}, u32[]{:S(2)}) collective-permute-start(bf16[4,60,120]{2,1,0:T(8,128)(2,1)S(1)} %pad_maximum_fusion), channel_id=1, source_target_pairs={{0,1},{1,0},{2,3},{3,2},{4,5},{5,4},{6,7},{7,6},{8,9},{9,8},{10,11... | collective-permute-start | bytes 172808 | tf_op jit(solution)/shard_map/ppermute | solution.py:192
  29.3 7.3 %collective-permute-start.2 = (bf16[4,60,120]{2,1,0:T(8,128)(2,1)S(1)}, bf16[4,60,120]{2,1,0:T(8,128)(2,1)S(1)}, u32[]{:S(2)}, u32[]{:S(2)}) collective-permute-start(bf16[4,60,120]{2,1,0:T(8,128)(2,1)S(1)} %get-tuple-element.9), channel_id=1, source_target_pairs={{0,4},{2,6},{4,8},{6,10},{8,12},{10,14},{12,16},{14,18},{16,20},{1... | collective-permute-start | bytes 172808 | tf_op jit(solution)/shard_map/ppermute | solution.py:184
  29.3 9.4 %collective-permute-start.3 = (bf16[4,60,120]{2,1,0:T(8,128)(2,1)S(1)}, bf16[4,60,120]{2,1,0:T(8,128)(2,1)S(1)}, u32[]{:S(2)}, u32[]{:S(2)}) collective-permute-start(bf16[4,60,120]{2,1,0:T(8,128)(2,1)S(1)} %get-tuple-element.10), channel_id=1, source_target_pairs={{0,5},{1,4},{2,7},{3,6},{4,9},{5,8},{6,11},{7,10},{8,13},{9,12},{1... | collective-permute-start | bytes 172808 | tf_op jit(solution)/shard_map/ppermute | solution.py:192
  29.3 9.4 %collective-permute-start.4 = (bf16[4,60,120]{2,1,0:T(8,128)(2,1)S(1)}, bf16[4,60,120]{2,1,0:T(8,128)(2,1)S(1)}, u32[]{:S(2)}, u32[]{:S(2)}) collective-permute-start(bf16[4,60,120]{2,1,0:T(8,128)(2,1)S(1)} %get-tuple-element.11), channel_id=1, source_target_pairs={{0,2},{2,4},{4,6},{6,8},{8,10},{10,12},{12,14},{14,16},{16,18},{18... | collective-permute-start | bytes 172808 | tf_op jit(solution)/shard_map/ppermute | solution.py:184
  30.9 7.8 %collective-permute-start.5 = (bf16[4,60,120]{2,1,0:T(8,128)(2,1)S(1)}, bf16[4,60,120]{2,1,0:T(8,128)(2,1)S(1)}, u32[]{:S(2)}, u32[]{:S(2)}) collective-permute-start(bf16[4,60,120]{2,1,0:T(8,128)(2,1)S(1)} %get-tuple-element.12), channel_id=1, source_target_pairs={{0,3},{1,2},{2,5},{3,4},{4,7},{5,6},{6,9},{7,8},{8,11},{9,10},{10,... | collective-permute-start | bytes 172808 | tf_op jit(solution)/shard_map/ppermute | solution.py:192

commit v6 on v5

--- a/solution.py
+++ b/solution.py
@@ -9,7 +9,6 @@
 F32, BF16 = jnp.float32, jnp.bfloat16
 SLAB = 128
 STEP = 2
-EARLY = 1
 
 
 def table_copies(pairs, ranks, pairs_s, ranks_s, sems):
@@ -74,7 +73,7 @@
     shard = block * lax.axis_size("aux") + lax.axis_index("aux")
     small = table_copies(pairs, ranks, pairs_s, ranks_s, small_sems)
     small.append(pltpu.make_async_copy(counts, counts_s, small_sems.at[2]))
-    small.append(pltpu.make_async_copy(amps.at[0:EARLY], amps_v, small_sems.at[3]))
+    small.append(pltpu.make_async_copy(amps, amps_v, small_sems.at[3]))
     copies = [pltpu.make_async_copy(panels.at[o], raw.at[o], sems.at[o]) for o in range(orbitals)]
     for copy in small + copies:
         copy.start()
@@ -93,7 +92,7 @@
             return carry
 
         lax.fori_loop(0, slots // 2, widen, 0, unroll=2)
-    work = [(block * owned + p, amps_v[p], stored(out, p)) for p in range(EARLY)]
+    work = [(block * owned + p, amps_v[p], stored(out, p)) for p in range(owned)]
     terms(work, paired, squares, pairs_s, ranks_s)
 
 
@@ -132,18 +131,19 @@
 
 def loaded(counts, pairs, ranks, amps, panels):
     orbitals, slots, width, _ = panels.shape
+    owned = amps.shape[0]
     return pl.pallas_call(
         load_body,
         out_shape=(
             pltpu.VMEM((orbitals, slots // 2, 2, SLAB, SLAB), BF16),
-            halves(EARLY, width, F32),
+            halves(owned, width, F32),
         ),
         in_specs=[in_place()] * 5,
         out_specs=(in_vmem(), in_vmem()),
         scratch_shapes=[
             pltpu.VMEM(panels.shape, BF16),
-            pltpu.VMEM((EARLY, width, width), BF16),
-            pltpu.VMEM((EARLY, SLAB, SLAB), BF16),
+            pltpu.VMEM(amps.shape, BF16),
+            pltpu.VMEM((owned, SLAB, SLAB), BF16),
             pltpu.SMEM(counts.shape, jnp.int32),
             pltpu.SMEM(pairs.shape, jnp.int32),
             pltpu.SMEM(ranks.shape, jnp.int32),
@@ -197,20 +197,18 @@
     ranks = pair_ranks
     far_amps = passed_along(amplitudes, "blk", -2)
     near_amps = passed_along(amplitudes, "blk", -1)
-    paired, early = loaded(
+    paired, own = loaded(
         kept_in_hbm(aux_counts), kept_in_hbm(pairs), kept_in_hbm(ranks), kept_in_hbm(amplitudes), kept_in_hbm(panels)
     )
-    far = group_terms(0, 2, BF16, pairs, ranks, far_amps, paired, early)
+    own_other = passed_across(own[1].astype(BF16), 0)
+    far = group_terms(0, 2, BF16, pairs, ranks, far_amps, paired, own)
     near = group_terms(0, 1, BF16, pairs, ranks, near_amps, paired, far)
-    late = group_terms(EARLY, 0, F32, pairs, ranks, amplitudes, paired, near)
+    far_other = passed_across(far[1], 2)
     far_same = passed_along(far[0], "blk", 2)
-    far_other = passed_across(far[1], 2)
+    near_other = passed_across(near[1], 1)
     near_same = passed_along(near[0], "blk", 1)
-    near_other = passed_across(near[1], 1)
-    own = jnp.concatenate([early[0], late[0]], axis=0)
-    own_other = passed_across(jnp.concatenate([early[1], late[1]], axis=0).astype(BF16), 0)
-    total = own
-    for part in (far_same, far_other, near_same, near_other, own_other):
+    total = own[0]
+    for part in (own_other, far_same, far_other, near_same, near_other):
         total = total + part.astype(F32)
     return total
 

time: 39.8 us -> 40.9 us (1.028)
  waiting for transfers between devices: 6.81 us -> 9.66 us
  Pallas kernels: 15.9 us -> 15.1 us
  starting transfers between devices: 15.8 us -> 15.2 us
    ppermute x3, waiting for transfers between devices: 2.07 us -> 6.45 us  [passed_across(): return lax.ppermute(value, ('blk', 'aux'), route)]
    pallas_call x3 -> x2, Pallas kernels: 11.2 us -> 7.98 us  [group_terms(): pl.pallas_call(functools.partial(group_body, first, hops), out_shape=halv...]
    pallas_call x1, Pallas kernels: 4.69 us -> 7.09 us  [loaded(): pl.pallas_call(load_body, out_shape=(pltpu.VMEM((orbitals, slots // 2, 2,...]
    ppermute x4, waiting for transfers between devices: 4.73 us -> 3.21 us  [passed_along(): lax.ppermute(value, axis, [(source, (source + steps) % count) for source...]
    ppermute x3, starting transfers between devices: 3.68 us -> 2.87 us  [passed_across(): return lax.ppermute(value, ('blk', 'aux'), route)]
  transfers between devices with their start and end apart: 7 -> 7, of which waited for: 2 -> 4; matrix products, arithmetic and copies ran while one was open for 0% -> 0% of each run, Pallas kernels for 22% -> 37%
where the time goes in v6:
time: 40.9 us; the launch traced here: 40.8 us
  starting transfers between devices  15.2 us (37%)
  Pallas kernels  15.1 us (37%)
  waiting for transfers between devices  9.66 us (24%)
  local copies, waits for them, and re-layouts  0.77 us (2%)
    ppermute x4, starting transfers between devices, passed_along(): lax.ppermute(value, axis, [(source, (source + steps) % count) for source...  12.3 us
    pallas_call x2, Pallas kernels, group_terms(): pl.pallas_call(functools.partial(group_body, first, hops), out_shape=halv...  7.98 us
    pallas_call x1, Pallas kernels, loaded(): pl.pallas_call(load_body, out_shape=(pltpu.VMEM((orbitals, slots // 2, 2,...  7.09 us
    ppermute x3, waiting for transfers between devices, passed_across(): return lax.ppermute(value, ('blk', 'aux'), route)  6.45 us
    ppermute x4, waiting for transfers between devices, passed_along(): lax.ppermute(value, axis, [(source, (source + steps) % count) for source...  3.21 us
    ppermute x3, starting transfers between devices, passed_across(): return lax.ppermute(value, ('blk', 'aux'), route)  2.87 us
  transfers between devices with their start and end apart: 7, of which 4 were waited for; matrix products, arithmetic and copies ran while one was open for 0% of the time, Pallas kernels for 37%

profile of v6, /device:TPU:1, one launch (start us, length us, event | category | flops | bytes accessed | tf_op | source)
XLA Modules:
  0.0 40.8 jit_solution(8037083132020059734)
XLA Ops:
  0.0 0.0 copy-start.1
  0.0 0.0 copy-start
  0.0 3.2 %collective-permute-start.4 = (bf16[4,120,120]{2,1,0:T(8,128)(2,1)}, bf16[4,120,120]{2,1,0:T(8,128)(2,1)S(1)}, u32[]{:S(2)}, u32[]{:S(2)}) collective-permute-start(bf16[4,120,120]{2,1,0:T(8,128)(2,1)} %amps.1), channel_id=1, source_target_pairs={{0,254},{2,0},{4,2},{6,4},{8,6},{10,8},{12,10},{14,12},{16,14},{18... | collective-permute-start | bytes 345608 | tf_op jit(solution)/shard_map/ppermute | solution.py:184
  3.2 7.2 %collective-permute-start.1 = (bf16[4,120,120]{2,1,0:T(8,128)(2,1)}, bf16[4,120,120]{2,1,0:T(8,128)(2,1)S(1)}, u32[]{:S(2)}, u32[]{:S(2)}) collective-permute-start(bf16[4,120,120]{2,1,0:T(8,128)(2,1)} %amps.1), channel_id=1, source_target_pairs={{0,252},{2,254},{4,0},{6,2},{8,4},{10,6},{12,8},{14,10},{16,12},{1... | collective-permute-start | bytes 345608 | tf_op jit(solution)/shard_map/ppermute | solution.py:184
  10.5 7.1 %loaded.1 = (bf16[4,22,2,128,128]{4,3,2,1,0:T(8,128)(2,1)S(1)}, f32[2,4,60,120]{3,2,1,0:T(8,128)S(1)}) custom-call(s32[256]{0:T(256)} %counts.1, s32[2,512]{1,0:T(2,128)} %bitcast.21, s32[512]{0:T(512)} %ranks.5, bf16[4,120,120]{2,1,0:T(8,128)(2,1)} %amps.1, bf16[4,44,120,120]{3,2,1,0:T(8,128)(2,1)} %panels.1), custom_call_target="tpu_custom_call" | custom-call | flops 3000000000 | bytes 5000000 | tf_op jit(solution)/shard_map/loaded/pallas_call | solution.py:135
  17.6 2.5 %collective-permute-start = (bf16[4,60,120]{2,1,0:T(8,128)(2,1)S(1)}, bf16[4,60,120]{2,1,0:T(8,128)(2,1)S(1)}, u32[]{:S(2)}, u32[]{:S(2)}) collective-permute-start(bf16[4,60,120]{2,1,0:T(8,128)(2,1)S(1)} %fusion.4), channel_id=1, source_target_pairs={{0,1},{1,0},{2,3},{3,2},{4,5},{5,4},{6,7},{7,6},{8,9},{9,8},{10,11... | collective-permute-start | bytes 172808 | tf_op jit(solution)/shard_map/ppermute | solution.py:192
  20.1 0.0 collective-permute-done.1.amps
  20.1 0.0 copy-done.1
  20.1 0.0 copy-done
  20.1 4.0 %shard_map.55.after = bf16[2,4,60,120]{3,2,1,0:T(8,128)(2,1)S(1)} custom-call(s32[2,512]{1,0:T(2,128)S(1)} %bitcast.22, s32[512]{0:T(512)S(1)} %copy-done.1, bf16[4,120,120]{2,1,0:T(8,128)(2,1)S(1)} %collective-permute-done.1.amps, bf16[4,22,2,128,128]{4,3,2,1,0:T(8,128)(2,1)S(1)} %get-tuple-element.8.paired, f32[2,4,60,120]{3,2,1,0:T(8,128)S(1)} %get-tuple-element.7.after), custom_call_target="tpu_custom_call" | custom-call | flops 4000000000 | bytes 5000000 | tf_op jit(solution)/shard_map/pallas_call | solution.py:171
  24.1 0.0 collective-permute-done.4.amps
  24.1 4.0 %shard_map.56 = bf16[2,4,60,120]{3,2,1,0:T(8,128)(2,1)S(1)} custom-call(s32[2,512]{1,0:T(2,128)S(1)} %bitcast.23, s32[512]{0:T(512)S(1)} %copy-done.1, bf16[4,120,120]{2,1,0:T(8,128)(2,1)S(1)} %collective-permute-done.4.amps, bf16[4,22,2,128,128]{4,3,2,1,0:T(8,128)(2,1)S(1)} %get-tuple-element.8.paired, bf16[2,4,60,120]{3,2,1,0:T(8,128)(2,1)S(1)} %shard_map.55.after), custom_call_target="tpu_custom_call" | custom-call | flops 4000000000 | bytes 5000000 | tf_op jit(solution)/shard_map/pallas_call | solution.py:171
  28.2 1.9 %collective-permute-start.5 = (bf16[4,60,120]{2,1,0:T(8,128)(2,1)S(1)}, bf16[4,60,120]{2,1,0:T(8,128)(2,1)S(1)}, u32[]{:S(2)}, u32[]{:S(2)}) collective-permute-start(bf16[4,60,120]{2,1,0:T(8,128)(2,1)S(1)} %get-tuple-element.11), channel_id=1, source_target_pairs={{0,2},{2,4},{4,6},{6,8},{8,10},{10,12},{12,14},{14,16},{16,18},{18... | collective-permute-start | bytes 172808 | tf_op jit(solution)/shard_map/ppermute | solution.py:184
  30.1 0.3 collective-permute-start.6
  30.4 0.0 collective-permute-start.2
  30.4 0.0 collective-permute-start.3
  30.4 0.0 collective-permute-done
  30.4 1.0 %collective-permute-done.5 = bf16[4,60,120]{2,1,0:T(8,128)(2,1)S(1)} collective-permute-done((bf16[4,60,120]{2,1,0:T(8,128)(2,1)S(1)}, bf16[4,60,120]{2,1,0:T(8,128)(2,1)S(1)}, u32[]{:S(2)}, u32[]{:S(2)}) %collective-permute-start.5) | collective-permute-done | bytes 57632 | tf_op jit(solution)/shard_map/ppermute | solution.py:184
  31.4 4.8 %collective-permute-done.6 = bf16[4,60,120]{2,1,0:T(8,128)(2,1)S(1)} collective-permute-done((bf16[4,60,120]{2,1,0:T(8,128)(2,1)S(1)}, bf16[4,60,120]{2,1,0:T(8,128)(2,1)S(1)}, u32[]{:S(2)}, u32[]{:S(2)}) %collective-permute-start.6) | collective-permute-done | bytes 57632 | tf_op jit(solution)/shard_map/ppermute | solution.py:192
  36.2 2.2 %collective-permute-done.2 = bf16[4,60,120]{2,1,0:T(8,128)(2,1)S(1)} collective-permute-done((bf16[4,60,120]{2,1,0:T(8,128)(2,1)S(1)}, bf16[4,60,120]{2,1,0:T(8,128)(2,1)S(1)}, u32[]{:S(2)}, u32[]{:S(2)}) %collective-permute-start.2) | collective-permute-done | bytes 57632 | tf_op jit(solution)/shard_map/ppermute | solution.py:184
  38.4 1.7 %collective-permute-done.3 = bf16[4,60,120]{2,1,0:T(8,128)(2,1)S(1)} collective-permute-done((bf16[4,60,120]{2,1,0:T(8,128)(2,1)S(1)}, bf16[4,60,120]{2,1,0:T(8,128)(2,1)S(1)}, u32[]{:S(2)}, u32[]{:S(2)}) %collective-permute-start.3) | collective-permute-done | bytes 57632 | tf_op jit(solution)/shard_map/ppermute | solution.py:192
  40.0 0.1 fusion.3
  40.1 0.7 %copy.6 = f32[4,60,120]{2,0,1:T(4,128)} copy(f32[4,60,120]{2,1,0:T(8,128)S(1)} %fusion.3) | data formatting | bytes 230400 | tf_op jit(solution)/shard_map/add | solution.py:212
  (3 shorter events, 0.0 us)
Async XLA Ops:
  0.0 20.1 %copy-start.1 = (s32[512]{0:T(512)S(1)}, s32[512]{0:T(512)}, u32[]{:S(2)}) copy-start(s32[512]{0:T(512)} %ranks.5) | copy-start | bytes 6148
  0.0 20.1 %copy-start = (s32[512,2]{0,1:T(2,128)S(1)}, s32[512,2]{0,1:T(2,128)}, u32[]{:S(2)}) copy-start(s32[512,2]{0,1:T(2,128)} %param.7) | copy-start | bytes 12292
  0.0 24.1 %collective-permute-start.4 = (bf16[4,120,120]{2,1,0:T(8,128)(2,1)}, bf16[4,120,120]{2,1,0:T(8,128)(2,1)S(1)}, u32[]{:S(2)}, u32[]{:S(2)}) collective-permute-start(bf16[4,120,120]{2,1,0:T(8,128)(2,1)} %amps.1), channel_id=1, source_target_pairs={{0,254},{2,0},{4,2},{6,4},{8,6},{10,8},{12,10},{14,12},{16,14},{18... | collective-permute-start | bytes 345608 | tf_op jit(solution)/shard_map/ppermute | solution.py:184
  3.2 16.9 %collective-permute-start.1 = (bf16[4,120,120]{2,1,0:T(8,128)(2,1)}, bf16[4,120,120]{2,1,0:T(8,128)(2,1)S(1)}, u32[]{:S(2)}, u32[]{:S(2)}) collective-permute-start(bf16[4,120,120]{2,1,0:T(8,128)(2,1)} %amps.1), channel_id=1, source_target_pairs={{0,252},{2,254},{4,0},{6,2},{8,4},{10,6},{12,8},{14,10},{16,12},{1... | collective-permute-start | bytes 345608 | tf_op jit(solution)/shard_map/ppermute | solution.py:184
  17.6 12.8 %collective-permute-start = (bf16[4,60,120]{2,1,0:T(8,128)(2,1)S(1)}, bf16[4,60,120]{2,1,0:T(8,128)(2,1)S(1)}, u32[]{:S(2)}, u32[]{:S(2)}) collective-permute-start(bf16[4,60,120]{2,1,0:T(8,128)(2,1)S(1)} %fusion.4), channel_id=1, source_target_pairs={{0,1},{1,0},{2,3},{3,2},{4,5},{5,4},{6,7},{7,6},{8,9},{9,8},{10,11... | collective-permute-start | bytes 172808 | tf_op jit(solution)/shard_map/ppermute | solution.py:192
  28.2 3.2 %collective-permute-start.5 = (bf16[4,60,120]{2,1,0:T(8,128)(2,1)S(1)}, bf16[4,60,120]{2,1,0:T(8,128)(2,1)S(1)}, u32[]{:S(2)}, u32[]{:S(2)}) collective-permute-start(bf16[4,60,120]{2,1,0:T(8,128)(2,1)S(1)} %get-tuple-element.11), channel_id=1, source_target_pairs={{0,2},{2,4},{4,6},{6,8},{8,10},{10,12},{12,14},{14,16},{16,18},{18... | collective-permute-start | bytes 172808 | tf_op jit(solution)/shard_map/ppermute | solution.py:184
  30.1 6.1 %collective-permute-start.6 = (bf16[4,60,120]{2,1,0:T(8,128)(2,1)S(1)}, bf16[4,60,120]{2,1,0:T(8,128)(2,1)S(1)}, u32[]{:S(2)}, u32[]{:S(2)}) collective-permute-start(bf16[4,60,120]{2,1,0:T(8,128)(2,1)S(1)} %get-tuple-element.12), channel_id=1, source_target_pairs={{0,3},{1,2},{2,5},{3,4},{4,7},{5,6},{6,9},{7,8},{8,11},{9,10},{10,... | collective-permute-start | bytes 172808 | tf_op jit(solution)/shard_map/ppermute | solution.py:192
  30.4 8.0 %collective-permute-start.2 = (bf16[4,60,120]{2,1,0:T(8,128)(2,1)S(1)}, bf16[4,60,120]{2,1,0:T(8,128)(2,1)S(1)}, u32[]{:S(2)}, u32[]{:S(2)}) collective-permute-start(bf16[4,60,120]{2,1,0:T(8,128)(2,1)S(1)} %get-tuple-element.9), channel_id=1, source_target_pairs={{0,4},{2,6},{4,8},{6,10},{8,12},{10,14},{12,16},{14,18},{16,20},{1... | collective-permute-start | bytes 172808 | tf_op jit(solution)/shard_map/ppermute | solution.py:184
  30.4 9.7 %collective-permute-start.3 = (bf16[4,60,120]{2,1,0:T(8,128)(2,1)S(1)}, bf16[4,60,120]{2,1,0:T(8,128)(2,1)S(1)}, u32[]{:S(2)}, u32[]{:S(2)}) collective-permute-start(bf16[4,60,120]{2,1,0:T(8,128)(2,1)S(1)} %get-tuple-element.10), channel_id=1, source_target_pairs={{0,5},{1,4},{2,7},{3,6},{4,9},{5,8},{6,11},{7,10},{8,13},{9,12},{1... | collective-permute-start | bytes 172808 | tf_op jit(solution)/shard_map/ppermute | solution.py:192
